TPU v7x, 32 devices: a 4x4x1 block of a 4x4x8 slice. The times are simulated.
32 devices in a mesh: dp: 1 (over z), fsdp: 32 (over y, x, core).
Axes of the slice: x: 4, y: 4, z: 1, core: 2. Of those that a mesh axis runs over, the one named last changes fastest.
The devices are a block of a 4x4x8 slice.
Arguments:
- tokens: bfloat16 [64, 64, 4096], P(('dp', 'fsdp'))
- k_cache: bfloat16 [64, 4096, 8, 128], P(('dp', 'fsdp'))
- v_cache: bfloat16 [64, 4096, 8, 128], P(('dp', 'fsdp'))
- prefix_len: int32 [64], P(('dp', 'fsdp'))
- rope_cos: float32 [64, 64, 64], P(('dp', 'fsdp'))
- rope_sin: float32 [64, 64, 64], P(('dp', 'fsdp'))
- norm_attn: bfloat16 [4096], P('fsdp')
- w_qkv: bfloat16 [4096, 6144], P('fsdp')
- b_qkv: bfloat16 [6144], P('fsdp')
- sink_logits: float32 [32], replicated
- w_out: bfloat16 [4096, 4096], P('fsdp')
- b_out: bfloat16 [4096], P('fsdp')
- norm_router: bfloat16 [4096], P('fsdp')
- w_router: bfloat16 [4096, 8], P('fsdp')
- b_router: float32 [8], replicated
Outputs:
- output 1: bfloat16 [64, 64, 4096], P(('dp', 'fsdp'))
- output 2: float32 [64, 64, 8], P(('dp', 'fsdp'))
- output 3: bfloat16 [64, 64, 8, 128], P(('dp', 'fsdp'))
- output 4: bfloat16 [64, 64, 8, 128], P(('dp', 'fsdp'))
All inputs are finite; a program needn't handle non-finite values.
Results may differ from a plain program's by a relative error of at most 0.00187.
Values are sent between devices in bfloat16 or wider.
A program may use at most 768 MiB of HBM per device.

v0:
```python
import jax
import jax.numpy as jnp
from jax import lax
from jax.sharding import PartitionSpec as P

NORM_EPS = 1e-5


def rms_scale(values, gain_vec):
    val_f32 = values.astype(jnp.float32)
    inv_rms = lax.rsqrt(jnp.mean(val_f32 * val_f32, axis=-1, keepdims=True) + NORM_EPS)
    return (val_f32 * inv_rms * gain_vec.astype(jnp.float32)).astype(jnp.bfloat16)


def apply_rope(values, cos_tab, sin_tab):
    half_dim = values.shape[-1] // 2
    first_half = values[..., :half_dim]
    second_half = values[..., half_dim:]
    return jnp.concatenate([first_half * cos_tab - second_half * sin_tab, second_half * cos_tab + first_half * sin_tab], axis=-1)


def attend_one(q_block, k_prev, v_prev, k_cur, v_cur, prev_len, head_sinks):
    n_new, n_kv, n_group, head_dim = q_block.shape
    n_prev = k_prev.shape[0]
    score_scale = head_dim ** -0.5
    s_prev = jnp.einsum('ckgd,pkd->kgcp', q_block, k_prev, preferred_element_type=jnp.float32) * score_scale
    s_cur = jnp.einsum('ckgd,jkd->kgcj', q_block, k_cur, preferred_element_type=jnp.float32) * score_scale
    s_prev = jnp.where(jnp.arange(n_prev) < prev_len, s_prev, -1e30)
    s_cur = jnp.where(jnp.arange(n_new)[None, :] <= jnp.arange(n_new)[:, None], s_cur, -1e30)
    sink_col = head_sinks.astype(jnp.float32).reshape(n_kv, n_group, 1, 1)
    row_max = jnp.maximum(jnp.maximum(jnp.max(s_prev, axis=-1, keepdims=True), jnp.max(s_cur, axis=-1, keepdims=True)), sink_col)
    p_prev = jnp.exp(s_prev - row_max)
    p_cur = jnp.exp(s_cur - row_max)
    denominator = jnp.sum(p_prev, axis=-1) + jnp.sum(p_cur, axis=-1) + jnp.exp(sink_col - row_max)[..., 0]
    weighted = jnp.einsum('kgcp,pkd->ckgd', p_prev.astype(jnp.bfloat16), v_prev, preferred_element_type=jnp.float32) + jnp.einsum('kgcj,jkd->ckgd', p_cur.astype(jnp.bfloat16), v_cur, preferred_element_type=jnp.float32)
    return (weighted / jnp.transpose(denominator, (2, 0, 1))[..., None]).astype(jnp.bfloat16)


def attention_part(qkv_rows, n_req, rope_cos, rope_sin, k_cache, v_cache, prefix_len, sink_logits):
    n_tok = qkv_rows.shape[0]
    n_new = n_tok // n_req
    n_kv = k_cache.shape[2]
    head_dim = k_cache.shape[3]
    n_heads = sink_logits.shape[0]
    q_width = n_heads * head_dim
    kv_width = n_kv * head_dim
    cos_tab = rope_cos.reshape(n_tok, 1, head_dim // 2)
    sin_tab = rope_sin.reshape(n_tok, 1, head_dim // 2)
    q_rot = apply_rope(qkv_rows[:, :q_width].reshape(n_tok, n_heads, head_dim), cos_tab, sin_tab).astype(jnp.bfloat16)
    k_rot = apply_rope(qkv_rows[:, q_width:q_width + kv_width].reshape(n_tok, n_kv, head_dim), cos_tab, sin_tab).astype(jnp.bfloat16)
    v_rows = qkv_rows[:, q_width + kv_width:].astype(jnp.bfloat16)
    q_req = q_rot.reshape(n_req, n_new, n_kv, n_heads // n_kv, head_dim)
    k_req = k_rot.reshape(n_req, n_new, n_kv, head_dim)
    v_req = v_rows.reshape(n_req, n_new, n_kv, head_dim)
    attn_out = lax.map(lambda item_tuple: attend_one(item_tuple[0], item_tuple[1], item_tuple[2], item_tuple[3], item_tuple[4], item_tuple[5], sink_logits), (q_req, k_cache, v_cache, k_req, v_req, prefix_len))
    return attn_out.reshape(n_tok, q_width), k_req, v_req


def solution(mesh):
    row_spec = P(('dp', 'fsdp'))
    shard_spec = P('fsdp')
    whole_spec = P()

    def local_step(tokens, k_cache, v_cache, prefix_len, rope_cos, rope_sin, norm_attn, w_qkv, b_qkv, sink_logits, w_out, b_out, norm_router, w_router, b_router):
        gain_attn = lax.all_gather(norm_attn, 'fsdp', axis=0, tiled=True)
        full_qkv = lax.all_gather(w_qkv, 'fsdp', axis=0, tiled=True)
        bias_qkv = lax.all_gather(b_qkv, 'fsdp', axis=0, tiled=True)
        full_out = lax.all_gather(w_out, 'fsdp', axis=0, tiled=True)
        bias_out = lax.all_gather(b_out, 'fsdp', axis=0, tiled=True)
        gain_router = lax.all_gather(norm_router, 'fsdp', axis=0, tiled=True)
        full_router = lax.all_gather(w_router, 'fsdp', axis=0, tiled=True)
        n_req, n_new, model_dim = tokens.shape
        flat_tok = tokens.reshape(n_req * n_new, model_dim)
        qkv_rows = jnp.dot(rms_scale(flat_tok, gain_attn), full_qkv, preferred_element_type=jnp.float32) + bias_qkv.astype(jnp.float32)
        attn_flat, k_req, v_req = attention_part(qkv_rows, n_req, rope_cos, rope_sin, k_cache, v_cache, prefix_len, sink_logits)
        proj_out = jnp.dot(attn_flat, full_out, preferred_element_type=jnp.float32) + bias_out.astype(jnp.float32)
        new_resid = (flat_tok.astype(jnp.float32) + proj_out).astype(jnp.bfloat16)
        logits = jnp.dot(rms_scale(new_resid, gain_router), full_router, preferred_element_type=jnp.float32) + b_router
        return (new_resid.reshape(n_req, n_new, model_dim), logits.reshape(n_req, n_new, -1), k_req, v_req)

    in_specs = (row_spec, row_spec, row_spec, row_spec, row_spec, row_spec, shard_spec, shard_spec, shard_spec, whole_spec, shard_spec, shard_spec, shard_spec, shard_spec, whole_spec)
    out_specs = (row_spec, row_spec, row_spec, row_spec)
    return jax.shard_map(local_step, mesh=mesh, in_specs=in_specs, out_specs=out_specs, check_vma=False)
```

profile of v0, /device:TPU:97, one launch (start us, length us, event | category | flops | bytes accessed | tf_op | source)
XLA Modules:
  0.0 401.5 jit_solution(3682134735863292790)
XLA Ops:
  8.8 32.7 %all-gather = bf16[32,1,128]{2,1,0:T(2,128)(2,1)S(1)} all-gather(bf16[1,1,128]{2,1,0:T(2,128)(2,1)} %bitcast.140), channel_id=1, replica_groups=mesh['dp'=1,'fsdp'=32] {'fsdp'}, dimensions={0}, use_global_device_ids=true | all-gather | bytes 8448 | tf_op jit(solution)/shard_map/all_gather | solution.py:65
  43.9 49.2 %all-reduce = bf16[6144]{0:T(1024)(128)(2,1)S(1)} all-reduce(bf16[6144]{0:T(1024)(128)(2,1)S(1)} %dynamic-update-slice), channel_id=1, replica_groups=mesh['dp'=1,'fsdp'=32] {'fsdp'}, use_global_device_ids=true, to_apply=%add | all-reduce | flops 6144 | bytes 24576
  95.0 29.4 %all-gather.1 = bf16[32,1,128]{2,1,0:T(2,128)(2,1)S(1)} all-gather(bf16[1,1,128]{2,1,0:T(2,128)(2,1)} %bitcast.141), channel_id=1, replica_groups=mesh['dp'=1,'fsdp'=32] {'fsdp'}, dimensions={0}, use_global_device_ids=true | all-gather | bytes 8448 | tf_op jit(solution)/shard_map/all_gather | solution.py:69
  125.0 32.5 %all-gather.2 = bf16[32,1,128]{2,1,0:T(2,128)(2,1)S(1)} all-gather(bf16[1,1,128]{2,1,0:T(2,128)(2,1)} %bitcast.142), channel_id=1, replica_groups=mesh['dp'=1,'fsdp'=32] {'fsdp'}, dimensions={0}, use_global_device_ids=true | all-gather | bytes 8448 | tf_op jit(solution)/shard_map/all_gather | solution.py:70
  158.1 32.2 %all_gather.27 = bf16[4096,8]{0,1:T(8,128)(2,1)} all-gather(bf16[128,8]{0,1:T(8,128)(2,1)} %param.30), channel_id=1, replica_groups=mesh['dp'=1,'fsdp'=32] {'fsdp'}, dimensions={0}, use_global_device_ids=true | all-gather | bytes 67584 | tf_op jit(solution)/shard_map/all_gather | solution.py:71
  190.3 2.5 fusion.31
  192.9 19.1 %convolution_add_fusion.1 = f32[128,6144]{1,0:T(8,128)S(1)} fusion(bf16[128,4096]{1,0:T(8,128)(2,1)} %fusion.31, bf16[4096,6144]{1,0:T(8,128)(2,1)} %all-gather.6.cloned.1.call-done, f32[6144]{0:T(1024)S(1)} %convert_element_type.53), kind=kOutput, calls=%fused_computation.42 | convolution fusion | flops 6443237376 | bytes 54550528 | tf_op jit(solution)/shard_map/dot_general | solution.py:74
  214.6 2.9 copy.54
  217.5 2.9 subtract_convert_fusion
  220.4 3.2 concatenate.18
  223.6 3.2 concatenate.19
  226.8 6.1 %pad_maximum_fusion = bf16[2,64,8,4,128]{1,0,4,3,2:T(2,128)(2,1)} fusion(bf16[2,64,8,4,64]{1,0,4,3,2:T(2,128)(2,1)} %concatenate.19, bf16[2,64,8,4,64]{1,0,4,3,2:T(2,128)(2,1)} %concatenate.18), kind=kLoop, calls=%fused_computation.51 | loop fusion | flops 524288 | bytes 2097152 | tf_op jit(solution)/shard_map/concatenate | solution.py:19
  232.9 4.7 %copy.44 = bf16[2,64,8,4,128]{4,1,3,2,0:T(8,128)(2,1)S(1)} copy(bf16[2,64,8,4,128]{1,0,4,3,2:T(2,128)(2,1)} %pad_maximum_fusion) | data formatting | bytes 2097152 | tf_op jit(solution)/shard_map/while | solution.py:55
  241.1 134.5 %while.10 = (s32[]{:T(128)}, bf16[2,64,8,4,128]{4,3,2,1,0:T(4,128)(2,1)}, bf16[2,4096,8,128]{3,2,1,0:T(8,128)(2,1)}, s32[2]{0:T(128)S(1)}, bf16[2,4096,8,128]{3,...) while((s32[]{:T(128)}, ...), condition=%wide.region_6.7_spmd, body=%wide.region_1.6_spmd.sunk | while | flops 4456065024 | bytes 158233728 | solution.py:55
  241.3 11.4 %constant_dynamic-slice_fusion.6 = (bf16[1,4096,8,128]{3,2,1,0:T(8,128)(2,1)}, bf16[1,4096,8,128]{3,2,1,0:T(8,128)(2,1)}) fusion(bf16[2,4096,8,128]{3,2,1,0:T(8,128)(2,1)} %get-tuple-element.218, s32[]{:T(128)} %get-tuple-element.204, bf16[2,4096,8,128]{3,2,1,0:T(8,128)(2,1)} %get-tuple-element.216), kind=kLoop, calls=%fused_computation.38.clone.1 | loop fusion | bytes 33554436 | tf_op jit(solution)/shard_map/while/body/jit(dynamic_index_in_dim)/dynamic_slice | solution.py:55
  253.9 17.0 %bitcast_reduce_fusion.2 = (f32[8,4,64]{2,1,0:T(4,128)}, f32[8,4096,64,4]{1,2,3,0:T(8,128)}) fusion(pred[4096]{0:T(1024)(128)(4,1)S(1)} %iota_compare_fusion.4, bf16[2,64,8,4,128]{4,1,3,2,0:T(8,128)(2,1)S(1)} %get-tuple-element.219, s32[]{:T(128)} %get-tuple-element.204, bf16[1,4096,8,128]{3,2,1,0:T(8,128)(2,1)} %get-tuple-element.186), kind=kOutput, calls=%fused_computation.1.clone.1 | convolution fusion | flops 2172647424 | bytes 42479620 | tf_op jit(solution)/shard_map/while/body/eval_jaxpr/ckgd,pkd->kgcp/dot_general | solution.py:26
  274.3 14.7 %fusion.53 = f32[8,4,64]{2,1,0:T(4,128)S(1)} fusion(f32[8,4096,64,4]{1,2,3,0:T(8,128)} %get-tuple-element.187, f32[8,4,64]{2,1,0:T(4,128)S(1)} %maximum_maximum_fusion.2, pred[4096]{0:T(1024)(128)(4,1)S(1)} %iota_compare_fusion.4), kind=kLoop, calls=%fused_computation.4.clone.1 | loop fusion | flops 33552384 | bytes 33574912 | tf_op jit(solution)/shard_map/while/body/eval_jaxpr/reduce_sum | solution.py:34
  289.1 17.6 %fusion.52 = f32[8,128,4,64]{1,3,2,0:T(8,128)S(1)} fusion(f32[8,4096,64,4]{1,2,3,0:T(8,128)} %get-tuple-element.187, f32[8,4,64]{2,1,0:T(4,128)S(1)} %maximum_maximum_fusion.2, pred[4096]{0:T(1024)(128)(4,1)S(1)} %iota_compare_fusion.4, bf16[1,4096,8,128]{3,2,1,0:T(8,128)(2,1)} %get-tuple-element.191), kind=kOutput, calls=%fused_computation.6.clone.1 | convolution fusion | flops 2181038080 | bytes 43003904 | tf_op jit(solution)/shard_map/while/body/eval_jaxpr/kgcp,pkd->ckgd/dot_general | solution.py:35
  308.5 11.3 %constant_dynamic-slice_fusion.6 = (bf16[1,4096,8,128]{3,2,1,0:T(8,128)(2,1)}, bf16[1,4096,8,128]{3,2,1,0:T(8,128)(2,1)}) fusion(bf16[2,4096,8,128]{3,2,1,0:T(8,128)(2,1)} %get-tuple-element.218, s32[]{:T(128)} %get-tuple-element.204, bf16[2,4096,8,128]{3,2,1,0:T(8,128)(2,1)} %get-tuple-element.216), kind=kLoop, calls=%fused_computation.38.clone.1 | loop fusion | bytes 33554436 | tf_op jit(solution)/shard_map/while/body/jit(dynamic_index_in_dim)/dynamic_slice | solution.py:55
  321.0 17.0 %bitcast_reduce_fusion.2 = (f32[8,4,64]{2,1,0:T(4,128)}, f32[8,4096,64,4]{1,2,3,0:T(8,128)}) fusion(pred[4096]{0:T(1024)(128)(4,1)S(1)} %iota_compare_fusion.4, bf16[2,64,8,4,128]{4,1,3,2,0:T(8,128)(2,1)S(1)} %get-tuple-element.219, s32[]{:T(128)} %get-tuple-element.204, bf16[1,4096,8,128]{3,2,1,0:T(8,128)(2,1)} %get-tuple-element.186), kind=kOutput, calls=%fused_computation.1.clone.1 | convolution fusion | flops 2172647424 | bytes 42479620 | tf_op jit(solution)/shard_map/while/body/eval_jaxpr/ckgd,pkd->kgcp/dot_general | solution.py:26
  341.4 14.7 %fusion.53 = f32[8,4,64]{2,1,0:T(4,128)S(1)} fusion(f32[8,4096,64,4]{1,2,3,0:T(8,128)} %get-tuple-element.187, f32[8,4,64]{2,1,0:T(4,128)S(1)} %maximum_maximum_fusion.2, pred[4096]{0:T(1024)(128)(4,1)S(1)} %iota_compare_fusion.4), kind=kLoop, calls=%fused_computation.4.clone.1 | loop fusion | flops 33552384 | bytes 33574912 | tf_op jit(solution)/shard_map/while/body/eval_jaxpr/reduce_sum | solution.py:34
  356.2 17.6 %fusion.52 = f32[8,128,4,64]{1,3,2,0:T(8,128)S(1)} fusion(f32[8,4096,64,4]{1,2,3,0:T(8,128)} %get-tuple-element.187, f32[8,4,64]{2,1,0:T(4,128)S(1)} %maximum_maximum_fusion.2, pred[4096]{0:T(1024)(128)(4,1)S(1)} %iota_compare_fusion.4, bf16[1,4096,8,128]{3,2,1,0:T(8,128)(2,1)} %get-tuple-element.191), kind=kOutput, calls=%fused_computation.6.clone.1 | convolution fusion | flops 2181038080 | bytes 43003904 | tf_op jit(solution)/shard_map/while/body/eval_jaxpr/kgcp,pkd->ckgd/dot_general | solution.py:35
  375.6 2.2 reshape.93
  377.8 15.6 %fusion.27 = (f32[128]{0:T(128)S(1)}, bf16[128,4096]{1,0:T(8,128)(2,1)S(1)}) fusion(f32[4096]{0:T(1024)} %bitcast.137, bf16[128,4096]{1,0:T(8,128)(2,1)S(1)} %reshape.93, bf16[4096,4096]{1,0:T(8,128)(2,1)} %all-gather.8.cloned.1.call-done, bf16[128,4096]{1,0:T(8,128)(2,1)S(1)} %bitcast.127), kind=kOutput, calls=%fused_computation.48 | convolution fusion | flops 4298637312 | bytes 36717056 | tf_op jit(solution)/shard_map/dot_general | solution.py:76
  (73 shorter events, 27.1 us)
Async XLA Ops:
  7.2 185.7 %all-gather.6.cloned.1.call-start = ((), (), s32[]{:S(2)}) async-start(), calls=%async_computation | async-start | bytes 51904512 | tf_op jit(solution)/shard_map/all_gather | solution.py:66
  8.0 369.8 %all-gather.8.cloned.1.call-start = ((), (), s32[]{:S(2)}) async-start(), calls=%async_computation.1 | async-start | bytes 34603008 | tf_op jit(solution)/shard_map/all_gather | solution.py:68
  212.0 14.8 %copy-start = (f32[128,6144]{1,0:T(8,128)}, f32[128,6144]{1,0:T(8,128)S(1)}, u32[]{:S(2)}) copy-start(f32[128,6144]{1,0:T(8,128)S(1)} %convolution_add_fusion.1) | copy-start | bytes 9437188
  217.5 21.9 %copy-start.4 = (f32[2,64,64]{2,1,0:T(8,128)S(1)}, f32[2,64,64]{2,1,0:T(8,128)}, u32[]{:S(2)}) copy-start(f32[2,64,64]{2,1,0:T(8,128)} %param.22) | copy-start | bytes 98308
  217.5 21.9 %copy-start.5 = (f32[2,64,64]{2,1,0:T(8,128)S(1)}, f32[2,64,64]{2,1,0:T(8,128)}, u32[]{:S(2)}) copy-start(f32[2,64,64]{2,1,0:T(8,128)} %param.21) | copy-start | bytes 98308
  217.5 23.5 %copy-start.8 = (f32[32]{0:T(128)S(1)}, f32[32]{0:T(128)}, u32[]{:S(2)}) copy-start(f32[32]{0:T(128)} %param.26) | copy-start | bytes 388
  217.5 23.5 %copy-start.9 = (s32[2]{0:T(128)S(1)}, s32[2]{0:T(128)}, u32[]{:S(2)}) copy-start(s32[2]{0:T(128)} %param.20) | copy-start | bytes 28
  241.1 136.7 %copy-start.1 = (bf16[2,64,4096]{2,1,0:T(8,128)(2,1)S(1)}, bf16[2,64,4096]{2,1,0:T(8,128)(2,1)}, u32[]{:S(2)}) copy-start(bf16[2,64,4096]{2,1,0:T(8,128)(2,1)} %param.17) | copy-start | bytes 3145732
  375.6 17.8 %copy-start.2 = (bf16[2,64,8,128]{3,2,1,0:T(8,128)(2,1)}, bf16[2,64,8,128]{3,2,1,0:T(8,128)(2,1)S(1)}, u32[]{:S(2)}) copy-start(bf16[2,64,8,128]{3,2,1,0:T(8,128)(2,1)S(1)} %get-tuple-element.228) | copy-start | bytes 786436
  377.8 15.6 %copy-start.6 = (bf16[4096,8]{0,1:T(8,128)(2,1)S(1)}, bf16[4096,8]{0,1:T(8,128)(2,1)}, u32[]{:S(2)}) copy-start(bf16[4096,8]{0,1:T(8,128)(2,1)} %all_gather.27) | copy-start | bytes 196612
  377.8 15.6 %copy-start.7 = (f32[32,1,128]{2,1,0:T(1,128)S(1)}, f32[32,1,128]{2,1,0:T(1,128)}, u32[]{:S(2)}) copy-start(f32[32,1,128]{2,1,0:T(1,128)} %convert_element_type.62) | copy-start | bytes 49156
  377.8 15.6 %copy-start.10 = (f32[8]{0:T(128)S(1)}, f32[8]{0:T(128)}, u32[]{:S(2)}) copy-start(f32[8]{0:T(128)} %param.31) | copy-start | bytes 100
  393.4 1.2 copy-start.3
Sparse Core Ops, SparseCore 0:
  10.1 158.3 all-gather.5
  170.6 107.2 all-gather.7
where the time goes:
time: 406 us; the launch traced here: 401 us
  blocking collectives  176 us (43%)
  matrix products  108 us (27%)
  local copies, waits for them, and re-layouts  52.3 us (13%)
  other arithmetic  49 us (12%)
  between operations  14.3 us (4%)
    unnamed x1, blocking collectives  49.2 us
    dot_general x2, matrix products, attend_one(): jnp.einsum('kgcp,pkd->ckgd', p_prev.astype(jnp.bfloat16), v_prev, preferr...  35.3 us
    dot_general x2, matrix products, attend_one(): jnp.einsum('ckgd,pkd->kgcp', q_block, k_prev, preferred_element_type=jnp....  34.1 us
    all_gather x1, blocking collectives, local_step(): gain_attn = lax.all_gather(norm_attn, 'fsdp', axis=0, tiled=True)  32.7 us
    all_gather x1, blocking collectives, local_step(): gain_router = lax.all_gather(norm_router, 'fsdp', axis=0, tiled=True)  32.5 us
    all_gather x1, blocking collectives, local_step(): full_router = lax.all_gather(w_router, 'fsdp', axis=0, tiled=True)  32.2 us
    reduce_sum x2, other arithmetic, attend_one(): jnp.sum(p_prev, axis=-1) + jnp.sum(p_cur, axis=-1)  29.4 us
    all_gather x1, blocking collectives, local_step(): bias_out = lax.all_gather(b_out, 'fsdp', axis=0, tiled=True)  29.4 us
  transfers between devices with their start and end apart: 2, of which 0 were waited for; matrix products, arithmetic and copies ran while one was open for 48% of the time, Pallas kernels for 0%

commit v1 on v0

v1 whole, which is shorter than its diff:
```python
import functools
import math

import jax
import jax.numpy as jnp
from jax import lax
from jax.experimental import pallas as pl
from jax.experimental.pallas import tpu as pltpu
from jax.sharding import PartitionSpec as P

NORM_EPS = 1e-5
AXIS = 'fsdp'
CORES = 2
MESH_ID = pl.DeviceIdType.MESH
BF16 = jnp.bfloat16
F32 = jnp.float32
LOG2E = 1.4426950408889634


class Place:
    def __init__(self, side):
        index = lax.axis_index(AXIS)
        self.side = side
        self.row = side * CORES
        self.c = lax.rem(index, CORES)
        self.x = lax.rem(index // CORES, side)
        self.y = index // self.row
        self.j = self.x * CORES + self.c

    def spot(self, dx, other=False):
        core = (1 - self.c) if other else self.c
        return lax.rem(self.x + dx, self.side) * CORES + core

    def line(self, dy):
        return lax.rem(self.y + dy, self.side)

    def mate(self, spot):
        return self.y * self.row + spot

    def above(self, dy):
        return self.line(dy) * self.row + self.j


class Sends:
    def __init__(self):
        self.started = []

    def __call__(self, src, dst, send_sem, recv_sem, device):
        copy = pltpu.make_async_remote_copy(
            src_ref=src, dst_ref=dst, send_sem=send_sem, recv_sem=recv_sem,
            device_id={AXIS: device}, device_id_type=MESH_ID)
        copy.start()
        self.started.append(copy)

    def finish(self):
        for copy in self.started:
            copy.wait_send()


def landed(ref, sem):
    pltpu.make_async_copy(ref, ref, sem).wait()


def meet(place):
    barrier = pltpu.get_barrier_semaphore()
    peers = [place.mate(place.spot(dx, other)) for dx in range(place.side) for other in (False, True) if dx or other]
    peers += [place.above(1), place.above(place.side - 1)]
    for peer in peers:
        pl.semaphore_signal(barrier, inc=1, device_id={AXIS: peer}, device_id_type=MESH_ID)
    pl.semaphore_wait(barrier, len(peers))


def rel_order(side):
    return [(0, True), (1, False), (side - 1, False), (1, True), (side - 1, True), (2, False), (2, True)]


class RowGather:
    def __init__(self, place, sends, buf, ring_s, ring_r, pair_s, pair_r):
        self.p, self.sends, self.buf = place, sends, buf
        self.ring_s, self.ring_r, self.pair_s, self.pair_r = ring_s, ring_r, pair_s, pair_r
        self.half = buf.shape[1] // 2

    def view(self, spot, h):
        return self.buf.at[spot, pl.ds(h * self.half, self.half)]

    def ring(self, spot, h, slot, dx):
        v = self.view(spot, h)
        self.sends(v, v, self.ring_s.at[slot], self.ring_r.at[slot], self.p.mate(self.p.spot(dx)))

    def pair(self, dx, h):
        v = self.view(self.p.spot(dx), h)
        slot = dx * 2 + h
        self.sends(v, v, self.pair_s.at[slot], self.pair_r.at[slot], self.p.mate(self.p.spot(0, True)))

    def start(self):
        p, back = self.p, self.p.side - 1
        self.ring(p.spot(0), 0, 0, 1)
        self.ring(p.spot(0), 1, 2, back)
        self.pair(0, 0)
        self.pair(0, 1)
        self.ring(p.spot(0), 1, 1, 1)
        self.ring(p.spot(0), 0, 3, back)

    def first(self):
        p, back = self.p, self.p.side - 1
        landed(self.view(p.spot(back), 0), self.ring_r.at[0])
        self.ring(p.spot(back), 0, 4, 1)
        self.pair(back, 0)
        landed(self.view(p.spot(1), 1), self.ring_r.at[2])
        self.ring(p.spot(1), 1, 5, back)
        self.pair(1, 1)

    def second(self):
        p, back = self.p, self.p.side - 1
        landed(self.view(p.spot(back), 1), self.ring_r.at[1])
        self.pair(back, 1)
        landed(self.view(p.spot(1), 0), self.ring_r.at[3])
        self.pair(1, 0)

    def third(self):
        p = self.p
        landed(self.view(p.spot(2), 0), self.ring_r.at[4])
        self.pair(2, 0)
        landed(self.view(p.spot(2), 1), self.ring_r.at[5])
        self.pair(2, 1)

    def from_pair(self, dx):
        for h in range(2):
            landed(self.view(self.p.spot(dx, True), h), self.pair_r.at[dx * 2 + h])


class ColumnGather:
    def __init__(self, place, sends, buf, up_s, up_r, down_s, down_r, far_s, far_r):
        self.p, self.sends, self.buf = place, sends, buf
        self.up_s, self.up_r, self.down_s, self.down_r = up_s, up_r, down_s, down_r
        self.far_s, self.far_r = far_s, far_r
        self.order = [(0, False)] + rel_order(place.side)

    def own(self, k):
        p = self.p
        v = self.buf.at[p.y, p.spot(*self.order[k])]
        self.sends(v, v, self.up_s.at[k], self.up_r.at[k], p.above(1))
        self.sends(v, v, self.down_s.at[k], self.down_r.at[k], p.above(p.side - 1))

    def near(self, k):
        p, back = self.p, self.p.side - 1
        spot = p.spot(*self.order[k])
        low, high = self.buf.at[p.line(back), spot], self.buf.at[p.line(1), spot]
        landed(low, self.up_r.at[k])
        if k % 2 == 0:
            self.sends(low, low, self.far_s.at[k], self.far_r.at[k], p.above(1))
        landed(high, self.down_r.at[k])
        if k % 2 == 1:
            self.sends(high, high, self.far_s.at[k], self.far_r.at[k], p.above(back))

    def far(self, k):
        p = self.p
        landed(self.buf.at[p.line(2), p.spot(*self.order[k])], self.far_r.at[k])


def dot_nt(a, b):
    return lax.dot_general(a, b, (((1,), (1,)), ((), ())), preferred_element_type=F32)


def project_kernel(side, heads, kv, w_ref, wo_ref, x_ref, cs_ref, pack_ref,
                   qkv_out, xb_out, pack_out, wo_out,
                   wl, wol, wq, xa, hh, csa, packs, acc, res, xbs,
                   s_wl, s_wol, s_loc, s_a2a, r_a2a, s_o, r_o, s_cs, r_cs, s_pk, r_pk, s_pv, r_pv,
                   s_ring, r_ring, s_pair, r_pair, s_up, r_up, s_dn, r_dn, s_far, r_far, s_res, r_res):
    p = Place(side)
    row = p.row
    back = side - 1
    head = w_ref.shape[1] // (heads + 2 * kv)
    qw = heads // kv * head
    depth = w_ref.shape[0]
    wide = qw + 2 * head
    rel = rel_order(side)
    sends = Sends()

    def take(spot, dst, sem):
        parts = ((spot * qw, qw, 0), (heads * head + spot * head, head, qw),
                 ((heads + kv) * head + spot * head, head, qw + head))
        for start, size, at in parts:
            pltpu.make_async_copy(w_ref.at[:, pl.ds(pl.multiple_of(start, head), size)],
                                  dst.at[:, pl.ds(at, size)], sem).start()

    take(p.j, wq.at[p.y, p.j], s_wl.at[0])
    for k, at in enumerate(rel):
        take(p.spot(*at), wl.at[k], s_wl.at[k + 1])
    pltpu.make_async_copy(x_ref, xa.at[p.j], s_loc.at[0]).start()
    ow = wol.shape[-1]
    for k, at in enumerate(rel):
        pltpu.make_async_copy(wo_ref.at[:, pl.ds(pl.multiple_of(p.spot(*at) * ow, head), ow)], wol.at[k],
                              s_wol.at[k]).start()
    own_o = pltpu.make_async_copy(wo_ref.at[:, pl.ds(pl.multiple_of(p.j * ow, head), ow)], wol.at[row - 1],
                                  s_wol.at[row - 1])
    own_o.start()
    packs[p.y, p.j] = pack_ref[...]
    csa[p.j] = cs_ref[...]

    meet(p)

    gather = ColumnGather(p, sends, wq, s_up, r_up, s_dn, r_dn, s_far, r_far)
    tokens = RowGather(p, sends, xa, s_ring, r_ring, s_pair, r_pair)
    landed(wq.at[p.y, p.j], s_wl.at[0])
    gather.own(0)
    for k, at in enumerate(rel):
        sends(pack_ref, packs.at[p.y, p.j], s_pk.at[k], r_pk.at[k], p.mate(p.spot(*at)))
    for k, at in enumerate(rel):
        landed(wl.at[k], s_wl.at[k + 1])
        sends(wl.at[k], wq.at[p.y, p.j], s_a2a.at[k], r_a2a.at[k], p.mate(p.spot(*at)))
    for k, at in enumerate(rel):
        sends(cs_ref, csa.at[p.j], s_cs.at[k], r_cs.at[k], p.mate(p.spot(*at)))
    landed(xa.at[p.j], s_loc.at[0])
    tokens.start()
    for k, at in enumerate(rel):
        landed(wol.at[k], s_wol.at[k])
        sends(wol.at[k], wo_out.at[p.j], s_o.at[k], r_o.at[k], p.mate(p.spot(*at)))
    own_o.wait()
    pltpu.make_async_copy(wol.at[row - 1], wo_out.at[p.j], s_loc.at[1]).start()

    def source(at):
        return p.spot(lax.rem(side - at[0], side) if at[0] else 0, at[1])

    def mirror(k):
        dx, other = rel[k]
        return rel.index(((side - dx) % side, other))

    for k in range(row - 1):
        landed(packs.at[p.y, p.spot(*rel[mirror(k)])], r_pk.at[k])
    pv = packs.at[p.y]
    sends(pv, pv, s_pv.at[0], r_pv.at[0], p.above(1))
    sends(pv, pv, s_pv.at[1], r_pv.at[1], p.above(back))
    for k in range(row - 1):
        m = mirror(k)
        landed(wq.at[p.y, p.spot(*rel[k])], r_a2a.at[m])
        gather.own(k + 1)
    pu = packs.at[p.line(back)]
    landed(pu, r_pv.at[0])
    sends(pu, pu, s_pv.at[2], r_pv.at[2], p.above(1))
    landed(packs.at[p.line(1)], r_pv.at[1])
    landed(packs.at[p.line(2)], r_pv.at[2])
    for k in range(row - 1):
        landed(csa.at[p.spot(*rel[mirror(k)])], r_cs.at[k])
    pltpu.make_async_copy(packs, pack_out, s_loc.at[2]).start()

    model = xa.shape[-1]
    xw = xbs.shape[-1]

    def norm(spot):
        xbs[spot] = xa[spot, :, pl.ds(pl.multiple_of(p.j * xw, head), xw)]
        total = jnp.zeros((xa.shape[1], head), F32)
        for i in range(model // head):
            v = xa[spot, :, i * head:(i + 1) * head].astype(F32)
            total = total + v * v
        inv = lax.rsqrt(jnp.sum(total, axis=-1, keepdims=True) / model + NORM_EPS)
        for i in range(model // head):
            v = xa[spot, :, i * head:(i + 1) * head].astype(F32)
            g = packs[i // row, i % row, 0:1, :]
            hh[spot, :, i * head:(i + 1) * head] = (v * inv * g).astype(BF16)

    span = row * depth

    def part(dx, dy):
        chip = lax.rem(p.x + dx, side)
        rows = hh[pl.ds(chip * CORES, CORES), :, pl.ds(pl.multiple_of(p.line(dy) * span, span), span)]
        rows = rows.reshape(CORES * hh.shape[1], span)
        return jnp.dot(rows, wq[p.line(dy)].reshape(span, wide), preferred_element_type=F32)

    def bias(m):
        e, k = m // 3, lax.rem(m, 3)
        out = 0.0
        for c in range(CORES):
            d = e * CORES + c
            out = out + packs[d // row, lax.rem(d, row), pl.ds(3 + k, 1), :]
        return out

    lanes = lax.broadcasted_iota(jnp.int32, (1, head), 1)

    def finish(dx):
        total = acc[dx] + part(dx, 2)
        chip = lax.rem(p.x + dx, side)
        cs = csa[pl.ds(chip * CORES, CORES)].reshape(CORES * csa.shape[1], head)
        turned = pltpu.roll(cs, head // 2, 1)
        low = lanes < head // 2
        cos = jnp.where(low, cs, turned)
        sin = jnp.where(low, -turned, cs)
        n_q = heads // kv
        for i in range(n_q + 2):
            m = p.j * n_q + i if i < n_q else (heads + p.j if i == n_q else heads + kv + p.j)
            t = total[:, i * head:(i + 1) * head] + bias(m)
            if i <= n_q:
                t = t * cos + pltpu.roll(t, head // 2, 1) * sin
            res[dx * CORES:(dx + 1) * CORES, :, i * head:(i + 1) * head] = t.astype(BF16).reshape(CORES, -1, head)
        for c in range(CORES):
            spot = chip * CORES + c
            src = res.at[dx * CORES + c]
            if dx:
                sends(src, qkv_out.at[p.j], s_res.at[dx * CORES + c], r_res.at[p.j], p.mate(spot))
            else:
                @pl.when(p.c == c)
                def _():
                    pltpu.make_async_copy(src, qkv_out.at[p.j], r_res.at[p.j]).start()

                @pl.when(p.c != c)
                def _():
                    pltpu.make_async_remote_copy(
                        src_ref=src, dst_ref=qkv_out.at[p.j], send_sem=s_res.at[0], recv_sem=r_res.at[p.j],
                        device_id={AXIS: p.mate(spot)}, device_id_type=MESH_ID).start()

    norm(p.spot(0))
    tokens.from_pair(0)
    norm(p.spot(0, True))
    tokens.first()
    for k in range(0, 4):
        gather.near(k)
    acc[0] = part(0, 0)
    tokens.second()
    for k in range(4, row):
        gather.near(k)
    acc[0] += part(0, 1)
    acc[0] += part(0, back)
    for dx in (back, 1):
        norm(p.spot(dx))
        tokens.from_pair(dx)
        norm(p.spot(dx, True))
        acc[dx] = part(dx, 0)
        acc[dx] += part(dx, 1)
        acc[dx] += part(dx, back)
    tokens.third()
    norm(p.spot(2))
    tokens.from_pair(2)
    norm(p.spot(2, True))
    xb = pltpu.make_async_copy(xbs, xb_out, s_loc.at[3])
    xb.start()
    for k in range(row):
        gather.far(k)
    finish(1)
    finish(back)
    acc[2] = part(2, 0)
    acc[2] += part(2, 1)
    acc[2] += part(2, back)
    finish(2)
    finish(0)
    for k in range(row - 1):
        landed(wo_out.at[p.spot(*rel[mirror(k)])], r_o.at[k])
    for i in range(row):
        landed(qkv_out.at[i], r_res.at[i])
    landed(wo_out.at[p.j], s_loc.at[1])
    landed(packs, s_loc.at[2])
    xb.wait()
    landed(res.at[0], s_res.at[0])
    sends.finish()


def attend_kernel(kv, len_ref, sink_ref, qkv_ref, k_ref, v_ref, o_ref, kb, vb, kt, vt, acc, top, low, s_k, s_v):
    n_req = k_ref.shape[0]
    head = k_ref.shape[-1]
    new = qkv_ref.shape[1] // n_req
    group = qkv_ref.shape[2] // head - 2
    block = kb.shape[1]
    scale = head ** -0.5 * LOG2E
    rows = group * new

    def span(r):
        return pl.ds(pl.multiple_of(r * new, new), new)

    def query(r, i):
        return jnp.concatenate([qkv_ref[i, span(r), g * head:(g + 1) * head] for g in range(group)], axis=0)

    def request(r, carry):
        length = len_ref[r]
        count = (length + block - 1) // block

        def fetch(b, slot):
            return (pltpu.make_async_copy(k_ref.at[r, pl.ds(b * block, block)], kb.at[slot], s_k.at[slot]),
                    pltpu.make_async_copy(v_ref.at[r, pl.ds(b * block, block)], vb.at[slot], s_v.at[slot]))

        @pl.when(count > 0)
        def _():
            for copy in fetch(0, 0):
                copy.start()

        causal = (lax.rem(lax.broadcasted_iota(jnp.int32, (rows, new), 0), new)
                  >= lax.broadcasted_iota(jnp.int32, (rows, new), 1))
        for i in range(kv):
            k_new = qkv_ref[i, span(r), group * head:(group + 1) * head]
            v_new = qkv_ref[i, span(r), (group + 1) * head:]
            s = jnp.where(causal, dot_nt(query(r, i), k_new) * scale, -1e30)
            sink = jnp.concatenate([jnp.full((new, head), sink_ref[i * group + g] * LOG2E, F32) for g in range(group)], axis=0)
            m = jnp.maximum(jnp.max(s, axis=-1, keepdims=True), sink)
            pr = jnp.exp2(s - m[:, :1])
            low[i] = jnp.sum(pr, axis=-1, keepdims=True) + jnp.exp2(sink - m)
            top[i] = m
            acc[i] = jnp.dot(pr.astype(BF16), v_new, preferred_element_type=F32)

        def step(b, _):
            slot = lax.rem(b, 2)

            @pl.when(b + 1 < count)
            def _():
                for copy in fetch(b + 1, 1 - slot):
                    copy.start()

            for copy in fetch(b, slot):
                copy.wait()
            kt[...] = pltpu.einshape('skd->ksd', kb[slot])
            vt[...] = pltpu.einshape('skd->ksd', vb[slot])
            limit = length - b * block

            def heads(masked):
                for i in range(kv):
                    s = dot_nt(query(r, i), kt[i]) * scale
                    if masked:
                        s = jnp.where(lax.broadcasted_iota(jnp.int32, (1, block), 1) < limit, s, -1e30)
                    m_old = top[i]
                    m = jnp.maximum(m_old, jnp.max(s, axis=-1, keepdims=True))
                    pr = jnp.exp2(s - m[:, :1])
                    fade = jnp.exp2(m_old - m)
                    low[i] = low[i] * fade + jnp.sum(pr, axis=-1, keepdims=True)
                    top[i] = m
                    acc[i] = acc[i] * fade + jnp.dot(pr.astype(BF16), vt[i], preferred_element_type=F32)

            @pl.when(limit >= block)
            def _():
                heads(False)

            @pl.when(limit < block)
            def _():
                heads(True)
            return 0

        lax.fori_loop(0, count, step, 0)
        for i in range(kv):
            out = (acc[i] / low[i]).astype(BF16)
            for g in range(group):
                at = (i * group + g) * head
                o_ref[span(r), at:at + head] = out[g * new:(g + 1) * new]
        return carry

    lax.fori_loop(0, n_req, request, 0)


def output_kernel(side, experts, o_ref, wo_ref, xb_ref, packs, br_ref, resid_out, logit_out,
                  oa, wq, xbv, acc, res, own,
                  s_loc, s_ring, r_ring, s_pair, r_pair, s_up, r_up, s_dn, r_dn, s_far, r_far, s_res, r_res):
    p = Place(side)
    row = p.row
    back = side - 1
    head = packs.shape[-1]
    depth = wq.shape[2]
    wide = wq.shape[3]
    sends = Sends()
    loads = [pltpu.make_async_copy(wo_ref, wq.at[p.y], s_loc.at[0]),
             pltpu.make_async_copy(o_ref, oa.at[p.j], s_loc.at[1]),
             pltpu.make_async_copy(xb_ref, xbv, s_loc.at[2])]
    for copy in loads:
        copy.start()
    meet(p)
    gather = ColumnGather(p, sends, wq, s_up, r_up, s_dn, r_dn, s_far, r_far)
    tokens = RowGather(p, sends, oa, s_ring, r_ring, s_pair, r_pair)
    loads[1].wait()
    tokens.start()
    loads[0].wait()
    for k in range(row):
        gather.own(k)
    loads[2].wait()
    span = row * depth

    def part(dx, dy):
        chip = lax.rem(p.x + dx, side)
        rows = oa[pl.ds(chip * CORES, CORES), :, pl.ds(pl.multiple_of(p.line(dy) * span, span), span)]
        rows = rows.reshape(CORES * oa.shape[1], span)
        return jnp.dot(rows, wq[p.line(dy)].reshape(span, wide), preferred_element_type=F32)

    def finish(dx):
        total = acc[dx] + part(dx, 2)
        chip = lax.rem(p.x + dx, side)
        for i in range(wide // head):
            d = p.j * (wide // head) + i
            b = packs[d // row, lax.rem(d, row), 1:2, :]
            at = pl.ds(i * head, head)
            base = xbv[pl.ds(chip * CORES, CORES), :, at].reshape(-1, head).astype(F32)
            t = base + (total[:, i * head:(i + 1) * head] + b)
            res[dx * CORES:(dx + 1) * CORES, :, at] = t.astype(BF16).reshape(CORES, -1, head)
        for c in range(CORES):
            spot = chip * CORES + c
            src = res.at[dx * CORES + c]
            if dx:
                sends(src, own.at[p.j], s_res.at[dx * CORES + c], r_res.at[p.j], p.mate(spot))
            else:
                @pl.when(p.c == c)
                def _():
                    own[p.j] = src[...]

                @pl.when(p.c != c)
                def _():
                    pltpu.make_async_remote_copy(
                        src_ref=src, dst_ref=own.at[p.j], send_sem=s_res.at[0], recv_sem=r_res.at[p.j],
                        device_id={AXIS: p.mate(spot)}, device_id_type=MESH_ID).start()

    tokens.from_pair(0)
    acc[0] = part(0, 0)
    tokens.first()
    for k in range(0, 4):
        gather.near(k)
    tokens.second()
    for k in range(4, row):
        gather.near(k)
    acc[0] += part(0, 1)
    acc[0] += part(0, back)
    for dx in (back, 1):
        tokens.from_pair(dx)
        acc[dx] = part(dx, 0)
        acc[dx] += part(dx, 1)
        acc[dx] += part(dx, back)
    tokens.third()
    for k in range(row):
        gather.far(k)
    finish(1)
    finish(back)
    tokens.from_pair(2)
    acc[2] = part(2, 0)
    acc[2] += part(2, 1)
    acc[2] += part(2, back)
    finish(2)
    finish(0)
    for dx, other in rel_order(side):
        spot = p.spot(dx, other)
        landed(own.at[spot], r_res.at[spot])
    n_tok = own.shape[1]
    model = row * wide
    outs = []
    for i in range(row):
        copy = pltpu.make_async_copy(own.at[i], resid_out.at[:, pl.ds(i * wide, wide)], s_loc.at[3 + i])
        copy.start()
        outs.append(copy)
    total = jnp.zeros((n_tok, head), F32)
    for i in range(row):
        for k in range(wide // head):
            v = own[i, :, k * head:(k + 1) * head].astype(F32)
            total = total + v * v
    inv = lax.rsqrt(jnp.sum(total, axis=-1, keepdims=True) / model + NORM_EPS)
    logits = jnp.zeros((n_tok, experts), F32)
    for i in range(row):
        for k in range(wide // head):
            d = i * (wide // head) + k
            v = own[i, :, k * head:(k + 1) * head].astype(F32)
            g = (v * inv * packs[d // row, d % row, 2:3, :]).astype(BF16)
            w = packs[d // row, d % row, 8:8 + experts, :].astype(BF16)
            logits = logits + dot_nt(g, w)
    logit_out[...] = logits + br_ref[...]
    for copy in outs:
        copy.wait()
    landed(res.at[0], s_res.at[0])
    sends.finish()


def dma(*shape):
    return pltpu.SemaphoreType.DMA(shape)


def solution(mesh):
    row_spec = P(('dp', 'fsdp'))
    shard_spec = P('fsdp')
    whole_spec = P()
    n_dev = mesh.shape[AXIS]
    side = math.isqrt(n_dev // CORES)
    row = side * CORES
    hbm = pl.BlockSpec(memory_space=pl.ANY)
    vmem = pl.BlockSpec(memory_space=pltpu.VMEM)
    smem = pl.BlockSpec(memory_space=pltpu.SMEM)

    def local_step(tokens, k_cache, v_cache, prefix_len, rope_cos, rope_sin, norm_attn, w_qkv, b_qkv, sink_logits, w_out, b_out, norm_router, w_router, b_router):
        n_req, n_new, model = tokens.shape
        kv, head = k_cache.shape[2:]
        heads = sink_logits.shape[0]
        experts = b_router.shape[0]
        depth = w_qkv.shape[0]
        n_tok = n_req * n_new
        wide = w_qkv.shape[1] // row
        ow = model // row
        flat = tokens.reshape(n_tok, model)
        cs = jnp.concatenate([rope_cos, rope_sin], axis=-1).reshape(n_tok, head)
        core = lax.rem(lax.axis_index(AXIS), CORES)
        bias_pad = lax.dynamic_update_slice(jnp.zeros((3 * head,), F32), b_qkv.astype(F32), (core * b_qkv.shape[0],))
        pack = jnp.concatenate([
            norm_attn.astype(F32)[None], b_out.astype(F32)[None], norm_router.astype(F32)[None],
            bias_pad.reshape(3, head), jnp.zeros((2, head), F32), w_router.astype(F32).T], axis=0)
        n_pack = pack.shape[0]

        qkv, xb, packs, wo = pl.pallas_call(
            functools.partial(project_kernel, side, heads, kv),
            out_shape=(jax.ShapeDtypeStruct((row, n_tok, wide), BF16),
                       jax.ShapeDtypeStruct((row, n_tok, ow), BF16),
                       jax.ShapeDtypeStruct((side, row, n_pack, head), F32),
                       jax.ShapeDtypeStruct((row, depth, ow), BF16)),
            in_specs=[hbm, hbm, hbm, vmem, vmem],
            out_specs=(hbm, hbm, hbm, hbm),
            scratch_shapes=[
                pltpu.VMEM((row - 1, depth, wide), BF16),
                pltpu.VMEM((row, depth, ow), BF16),
                pltpu.VMEM((side, row, depth, wide), BF16),
                pltpu.VMEM((row, n_tok, model), BF16),
                pltpu.VMEM((row, n_tok, model), BF16),
                pltpu.VMEM((row, n_tok, head), F32),
                pltpu.VMEM((side, row, n_pack, head), F32),
                pltpu.VMEM((side, CORES * n_tok, wide), F32),
                pltpu.VMEM((row, n_tok, wide), BF16),
                pltpu.VMEM((row, n_tok, ow), BF16),
                dma(row), dma(row), dma(4), dma(row), dma(row), dma(row), dma(row), dma(row), dma(row),
                dma(row), dma(row), dma(3), dma(3), dma(6), dma(6), dma(row), dma(row),
                dma(row), dma(row), dma(row), dma(row), dma(row), dma(row), dma(row), dma(row)],
            compiler_params=pltpu.CompilerParams(collective_id=0, has_side_effects=True, vmem_limit_bytes=60 * 2**20),
            name='project',
        )(w_qkv, w_out, flat, cs, pack)

        block = 512
        o = pl.pallas_call(
            functools.partial(attend_kernel, kv),
            out_shape=jax.ShapeDtypeStruct((n_tok, model), BF16),
            in_specs=[smem, smem, vmem, hbm, hbm],
            out_specs=vmem,
            scratch_shapes=[
                pltpu.VMEM((2, block, kv, head), BF16), pltpu.VMEM((2, block, kv, head), BF16),
                pltpu.VMEM((kv, block, head), BF16), pltpu.VMEM((kv, block, head), BF16),
                pltpu.VMEM((kv, heads // kv * n_new, head), F32), pltpu.VMEM((kv, heads // kv * n_new, head), F32),
                pltpu.VMEM((kv, heads // kv * n_new, head), F32), dma(2), dma(2)],
            compiler_params=pltpu.CompilerParams(vmem_limit_bytes=48 * 2**20),
            name='attend',
        )(prefix_len, sink_logits, qkv, k_cache, v_cache)

        resid, logits = pl.pallas_call(
            functools.partial(output_kernel, side, experts),
            out_shape=(jax.ShapeDtypeStruct((n_tok, model), BF16), jax.ShapeDtypeStruct((n_tok, experts), F32)),
            in_specs=[hbm, hbm, hbm, vmem, vmem],
            out_specs=(hbm, vmem),
            scratch_shapes=[
                pltpu.VMEM((row, n_tok, model), BF16),
                pltpu.VMEM((side, row, depth, ow), BF16),
                pltpu.VMEM((row, n_tok, ow), BF16),
                pltpu.VMEM((side, CORES * n_tok, ow), F32),
                pltpu.VMEM((row, n_tok, ow), BF16),
                pltpu.VMEM((row, n_tok, ow), BF16),
                dma(3 + row), dma(6), dma(6), dma(row), dma(row),
                dma(row), dma(row), dma(row), dma(row), dma(row), dma(row), dma(row), dma(row)],
            compiler_params=pltpu.CompilerParams(collective_id=1, has_side_effects=True, vmem_limit_bytes=48 * 2**20),
            name='output',
        )(o, wo, xb, packs, b_router.reshape(1, experts))

        split = qkv.reshape(row, n_req, n_new, wide)
        gw = wide - 2 * head
        k_new = jnp.transpose(split[..., gw:gw + head], (1, 2, 0, 3))
        v_new = jnp.transpose(split[..., gw + head:], (1, 2, 0, 3))
        return (resid.reshape(n_req, n_new, model), logits.reshape(n_req, n_new, experts), k_new, v_new)

    in_specs = (row_spec, row_spec, row_spec, row_spec, row_spec, row_spec, shard_spec, shard_spec, shard_spec, whole_spec, shard_spec, shard_spec, shard_spec, shard_spec, whole_spec)
    out_specs = (row_spec, row_spec, row_spec, row_spec)
    return jax.shard_map(local_step, mesh=mesh, in_specs=in_specs, out_specs=out_specs, check_vma=False)
```

time: 406 us -> 243 us (0.60); the launches traced: 401 us -> 243 us
  Pallas kernels: 0 us -> 232 us
  blocking collectives: 176 us -> 0 us
  matrix products: 108 us -> 0 us
  local copies, waits for them, and re-layouts: 52.3 us -> 5.82 us
  other arithmetic: 49 us -> 4.34 us
  between operations: 14.3 us -> 0.76 us
    pallas_call x0 -> x3, Pallas kernels: none -> 232 us  [the longest x1 102 us: local_step(): pl.pallas_call(functools.partial(project_kernel, side, heads, kv), out_sh...]
    all_gather x4 -> x0, blocking collectives: 127 us -> none  [the longest x1 32.7 us: local_step(): gain_attn = lax.all_gather(norm_attn, 'fsdp', axis=0, tiled=True)]
    dot_general x11 -> x0, matrix products: 108 us -> none  [the longest x2 35.3 us: attend_one(): jnp.einsum('kgcp,pkd->ckgd', p_prev.astype(jnp.bfloat16), v_prev, preferr...]
    unnamed x1 -> x0, blocking collectives: 49.2 us -> none
    reduce_sum x5 -> x0, other arithmetic: 31.4 us -> none  [the longest x2 29.4 us: attend_one(): jnp.sum(p_prev, axis=-1) + jnp.sum(p_cur, axis=-1)]
    dynamic_slice x6 -> x0, local copies, waits for them, and re-layouts: 25.7 us -> none  [attention_part(): lax.map(lambda item_tuple: attend_one(item_tuple[0], item_tuple[1], item_...]
    reshape x3 -> x0, local copies, waits for them, and re-layouts: 5.17 us -> none  [the longest x1 2.91 us: attention_part(): qkv_rows[:, :q_width].reshape(n_tok, n_heads, head_dim)]
    concatenate x2 -> x1, local copies, waits for them, and re-layouts: 6.36 us -> 1.2 us  [local_step(): jnp.concatenate([norm_attn.astype(F32)[None], b_out.astype(F32)[None], no...]
  transfers between devices with their start and end apart: 2 -> 0, of which waited for: 0 -> 0; matrix products, arithmetic and copies ran while one was open for 48% -> 0% of each run, Pallas kernels for 0% -> 0%
where the time goes in v1:
time: 243 us
  Pallas kernels  232 us (95%)
  local copies, waits for them, and re-layouts  5.82 us (2%)
  other arithmetic  4.34 us (2%)
    pallas_call x1, Pallas kernels, local_step(): pl.pallas_call(functools.partial(project_kernel, side, heads, kv), out_sh...  102 us
    pallas_call x1, Pallas kernels, local_step(): pl.pallas_call(functools.partial(output_kernel, side, experts), out_shape...  94.9 us
    pallas_call x1, Pallas kernels, local_step(): pl.pallas_call(functools.partial(attend_kernel, kv), out_shape=jax.ShapeD...  34.8 us

profile of v1, /device:TPU:97, one launch (start us, length us, event | category | flops | bytes accessed | tf_op | source)
XLA Modules:
  0.0 242.9 jit_solution(6848456371259421254)
XLA Ops:
  0.6 0.7 bitcast_convert_fusion.2
  1.3 0.7 bitcast_convert_fusion
  2.0 0.7 convert_dynamic-update-slice_fusion
  2.7 0.7 convert_bitcast_fusion
  3.4 1.2 concatenate.7.pack_ref
  4.6 1.6 pad_maximum_fusion
  6.2 102.3 %project.1 = (bf16[8,128,768]{2,1,0:T(8,128)(2,1)}, bf16[8,128,512]{2,1,0:T(8,128)(2,1)}, f32[4,8,16,128]{3,2,1,0:T(8,128)}, bf16[8,128,512]{2,1,0:T(8,128)(2,1)}) custom-call(bf16[128,6144]{1,0:T(8,128)(2,1)} %w_ref.1, bf16[128,4096]{1,0:T(8,128)(2,1)} %wo_ref.1, bf16[128,4096]{1,0:T(8,128)(2,1)} %bitcast.28, f32[128,128]{1,0:T(8,128)} %bitcast.29, ...), custom_call_target="tpu_custom_call" | custom-call | tf_op jit(solution)/shard_map/project/pallas_call | solution.py:592
  108.5 0.0 copy-start
  108.5 0.0 copy-start.5
  108.5 0.0 copy-start.6
  108.5 1.2 fusion
  109.7 0.9 copy.26
  110.6 0.9 copy.27
  111.5 0.0 copy-done
  111.5 0.0 copy-done.5
  111.5 0.0 copy-done.6
  111.5 0.0 copy-start.2
  111.5 0.0 copy-start.3
  111.5 0.0 copy-start.4
  111.5 34.8 %attend.1.o_ref = bf16[128,4096]{1,0:T(8,128)(2,1)S(1)} custom-call(s32[2]{0:T(128)S(1)} %copy-done.5, f32[32]{0:T(128)S(1)} %copy-done.6, bf16[8,128,768]{2,1,0:T(8,128)(2,1)S(1)} %copy-done, bf16[2,4096,8,128]{3,2,1,0:T(8,128)(2,1)} %k_ref.1, bf16[2,4096,8,128]{3,2,1,0:T(8,128)(2,1)} %v_ref.1), custom_call_target="tpu_custom_call" | custom-call | tf_op jit(solution)/shard_map/attend/pallas_call | solution.py:619
  146.3 0.0 copy-done.1
  146.3 94.9 %output.1 = (bf16[128,4096]{1,0:T(8,128)(2,1)S(1)}, f32[128,8]{1,0:T(8,128)S(1)}) custom-call(bf16[128,4096]{1,0:T(8,128)(2,1)S(1)} %attend.1.o_ref, bf16[8,128,512]{2,1,0:T(8,128)(2,1)S(1)} %copy-done.2, bf16[8,128,512]{2,1,0:T(8,128)(2,1)S(1)} %copy-done.1, f32[4,8,16,128]{3,2,1,0:T(8,128)S(1)} %copy-done.3, f32[1,8]{1,0:T(1,128)S(1)} %bitcast.27), custom_call_target="tpu_custom_call" | custom-call | tf_op jit(solution)/shard_map/output/pallas_call | solution.py:633
  241.3 0.7 copy.21
  241.9 1.0 copy.30
  (6 shorter events, 0.0 us)
Async XLA Ops:
  108.5 3.0 %copy-start = (bf16[8,128,768]{2,1,0:T(8,128)(2,1)S(1)}, bf16[8,128,768]{2,1,0:T(8,128)(2,1)}, u32[]{:S(2)}) copy-start(bf16[8,128,768]{2,1,0:T(8,128)(2,1)} %get-tuple-element.10.qkv_ref) | copy-start | bytes 4718596
  108.5 3.0 %copy-start.5 = (s32[2]{0:T(128)S(1)}, s32[2]{0:T(128)}, u32[]{:S(2)}) copy-start(s32[2]{0:T(128)} %len_ref.1) | copy-start | bytes 28
  108.5 3.0 %copy-start.6 = (f32[32]{0:T(128)S(1)}, f32[32]{0:T(128)}, u32[]{:S(2)}) copy-start(f32[32]{0:T(128)} %sink_ref.1) | copy-start | bytes 388
  111.5 34.8 %copy-start.1 = (bf16[8,128,512]{2,1,0:T(8,128)(2,1)S(1)}, bf16[8,128,512]{2,1,0:T(8,128)(2,1)}, u32[]{:S(2)}) copy-start(bf16[8,128,512]{2,1,0:T(8,128)(2,1)} %get-tuple-element.12.xb_ref) | copy-start | bytes 3145732
  111.5 34.8 %copy-start.2 = (bf16[8,128,512]{2,1,0:T(8,128)(2,1)S(1)}, bf16[8,128,512]{2,1,0:T(8,128)(2,1)}, u32[]{:S(2)}) copy-start(bf16[8,128,512]{2,1,0:T(8,128)(2,1)} %get-tuple-element.11.wo_ref) | copy-start | bytes 3145732
  111.5 34.8 %copy-start.3 = (f32[4,8,16,128]{3,2,1,0:T(8,128)S(1)}, f32[4,8,16,128]{3,2,1,0:T(8,128)}, u32[]{:S(2)}) copy-start(f32[4,8,16,128]{3,2,1,0:T(8,128)} %get-tuple-element.13.packs) | copy-start | bytes 786436
  111.5 34.8 %copy-start.4 = (f32[8]{0:T(128)S(1)}, f32[8]{0:T(128)}, u32[]{:S(2)}) copy-start(f32[8]{0:T(128)} %param.29) | copy-start | bytes 100

commit v2 on v1

v2 whole, which is shorter than its diff:
```python
import functools
import math

import jax
import jax.numpy as jnp
from jax import lax
from jax.experimental import pallas as pl
from jax.experimental.pallas import tpu as pltpu
from jax.sharding import PartitionSpec as P

NORM_EPS = 1e-5
AXIS = 'fsdp'
CORES = 2
MESH_ID = pl.DeviceIdType.MESH
BF16 = jnp.bfloat16
F32 = jnp.float32
LOG2E = 1.4426950408889634


class Place:
    def __init__(self, side, across=False):
        index = lax.axis_index(AXIS)
        self.side, self.across = side, across
        self.row = side * CORES
        self.c = lax.rem(index, CORES)
        x = lax.rem(index // CORES, side)
        y = index // self.row
        self.a, self.b = (y, x) if across else (x, y)
        self.j = self.a * CORES + self.c

    def device(self, a, b, c):
        return (a * self.side + b) * CORES + c if self.across else (b * self.side + a) * CORES + c

    def spot(self, da, other=False):
        core = (1 - self.c) if other else self.c
        return lax.rem(self.a + da, self.side) * CORES + core

    def line(self, db):
        return lax.rem(self.b + db, self.side)

    def mate(self, da, other=False):
        return self.device(lax.rem(self.a + da, self.side), self.b, (1 - self.c) if other else self.c)

    def above(self, db):
        return self.device(self.a, self.line(db), self.c)

    def mates(self):
        return [self.mate(da, other) for da in range(self.side) for other in (False, True) if da or other]


class Sends:
    def __init__(self):
        self.started = []

    def __call__(self, src, dst, send_sem, recv_sem, device, later=None):
        pltpu.make_async_remote_copy(
            src_ref=src, dst_ref=dst, send_sem=send_sem, recv_sem=recv_sem,
            device_id={AXIS: device}, device_id_type=MESH_ID).start()
        self.started.append(later or (lambda: (src, send_sem)))

    def finish(self):
        for later in self.started:
            landed(*later())


def landed(ref, sem):
    pltpu.make_async_copy(ref, ref, sem).wait()


def meet(peers):
    barrier = pltpu.get_barrier_semaphore()
    for peer in peers:
        pl.semaphore_signal(barrier, inc=1, device_id={AXIS: peer}, device_id_type=MESH_ID)
    pl.semaphore_wait(barrier, len(peers))


def rel_order(side):
    return [(0, True), (1, False), (side - 1, False), (1, True), (side - 1, True), (2, False), (2, True)]


def mirror(rel, k, side):
    da, other = rel[k]
    return rel.index(((side - da) % side, other))


class RowGather:
    def __init__(self, place, sends, view, count, plus, minus, far, pair):
        self.p, self.sends, self.view, self.count = place, sends, view, count
        self.plus, self.minus, self.far_sems, self.pair_sems = plus, minus, far, pair

    def go(self, spot, k, sems, slot, da, other=False):
        v = self.view(spot, k)
        self.sends(v, v, sems[0].at[slot], sems[1].at[slot], self.p.mate(da, other), lambda: (self.view(0, k), sems[0].at[slot]))

    def own(self, k):
        p = self.p
        self.go(p.j, k, self.plus, k, 1)
        self.go(p.j, k, self.minus, k, p.side - 1)
        self.go(p.j, k, self.pair_sems, k, 0, True)

    def near(self, k):
        p, back, n = self.p, self.p.side - 1, self.count
        low, high = p.spot(back), p.spot(1)
        landed(self.view(low, k), self.plus[1].at[k])
        if k % 2 == 0:
            self.go(low, k, self.far_sems, k, 1)
        self.go(low, k, self.pair_sems, n + k, 0, True)
        landed(self.view(high, k), self.minus[1].at[k])
        if k % 2 == 1:
            self.go(high, k, self.far_sems, k, back)
        self.go(high, k, self.pair_sems, 2 * n + k, 0, True)

    def far(self, k):
        spot = self.p.spot(2)
        landed(self.view(spot, k), self.far_sems[1].at[k])
        self.go(spot, k, self.pair_sems, 3 * self.count + k, 0, True)

    def from_pair(self, da):
        group = {0: 0, self.p.side - 1: 1, 1: 2, 2: 3}[da]
        for k in range(self.count):
            landed(self.view(self.p.spot(da, True), k), self.pair_sems[1].at[group * self.count + k])


class ColumnGather:
    def __init__(self, place, sends, buf, up, down, far):
        self.p, self.sends, self.buf = place, sends, buf
        self.up, self.down, self.far_sems = up, down, far
        self.order = [(0, False)] + rel_order(place.side)

    def go(self, line, k, sems, db):
        v = self.buf.at[line, self.p.spot(*self.order[k])]
        self.sends(v, v, sems[0].at[k], sems[1].at[k], self.p.above(db), lambda: (self.buf.at[0, 0], sems[0].at[k]))

    def own(self, k):
        self.go(self.p.b, k, self.up, 1)
        self.go(self.p.b, k, self.down, self.p.side - 1)

    def near(self, k):
        p, back = self.p, self.p.side - 1
        spot = p.spot(*self.order[k])
        landed(self.buf.at[p.line(back), spot], self.up[1].at[k])
        if k % 2 == 0:
            self.go(p.line(back), k, self.far_sems, 1)
        landed(self.buf.at[p.line(1), spot], self.down[1].at[k])
        if k % 2 == 1:
            self.go(p.line(1), k, self.far_sems, back)

    def far(self, k):
        landed(self.buf.at[self.p.line(2), self.p.spot(*self.order[k])], self.far_sems[1].at[k])


def dot_nt(a, b):
    return lax.dot_general(a, b, (((1,), (1,)), ((), ())), preferred_element_type=F32)


def project_kernel(side, heads, kv, w_ref, wo_ref, x_ref, cs_ref, pack_ref, k_ref, v_ref,
                   qkv_out, xb_out, pack_out, wo_out, kt_out, vt_out,
                   wl, wol, wq, xa, hh, csa, packs, acc, res, kin, vin, kmid, vmid,
                   s_wl, s_wol, s_loc, s_a2a, r_a2a, s_o, r_o, s_x, r_x, s_cs, r_cs, s_pk, r_pk, s_pv, r_pv,
                   s_plus, r_plus, s_minus, r_minus, s_rfar, r_rfar, s_pair, r_pair,
                   s_up, r_up, s_dn, r_dn, s_far, r_far, s_res, r_res, s_in, s_mid):
    p = Place(side)
    t = Place(side, across=True)
    row = p.row
    back = side - 1
    head = w_ref.shape[1] // (heads + 2 * kv)
    qw = heads // kv * head
    depth = w_ref.shape[0]
    wide = qw + 2 * head
    ow = wol.shape[-1]
    rel = rel_order(side)
    sends = Sends()

    def take(spot, dst, sem):
        parts = ((spot * qw, qw, 0), (heads * head + spot * head, head, qw),
                 ((heads + kv) * head + spot * head, head, qw + head))
        for start, size, at in parts:
            pltpu.make_async_copy(w_ref.at[:, pl.ds(pl.multiple_of(start, head), size)],
                                  dst.at[:, pl.ds(at, size)], sem).start()

    take(p.j, wq.at[p.b, p.j], s_wl.at[0])
    for k, at in enumerate(rel):
        take(p.spot(*at), wl.at[k], s_wl.at[k + 1])
    pltpu.make_async_copy(x_ref, xa.at[p.j], s_loc.at[0]).start()
    for k, at in enumerate(rel + [(0, False)]):
        pltpu.make_async_copy(wo_ref.at[:, pl.ds(pl.multiple_of(t.spot(*at) * ow, head), ow)], wol.at[k],
                              s_wol.at[k]).start()

    depth_in, block = kin.shape[0], kin.shape[1]
    per = k_ref.shape[1] // block
    steps = k_ref.shape[0] * per

    def bring(b, slot):
        r, at = b // per, lax.rem(b, per) * block
        return (pltpu.make_async_copy(k_ref.at[r, pl.ds(at, block)], kin.at[slot], s_in.at[slot]),
                pltpu.make_async_copy(v_ref.at[r, pl.ds(at, block)], vin.at[slot], s_in.at[depth_in + slot]))

    def put(b, slot):
        r, at = b // per, lax.rem(b, per) * block
        return (pltpu.make_async_copy(kmid.at[slot], kt_out.at[r, :, pl.ds(at, block)], s_mid.at[slot]),
                pltpu.make_async_copy(vmid.at[slot], vt_out.at[r, :, pl.ds(at, block)], s_mid.at[depth_in + slot]))

    def turn(b, _):
        slot = lax.rem(b, depth_in)
        for copy in bring(b, slot):
            copy.wait()

        @pl.when(b >= depth_in)
        def _():
            for copy in put(b - depth_in, slot):
                copy.wait()
        kmid[slot] = pltpu.einshape('skd->ksd', kin[slot])
        vmid[slot] = pltpu.einshape('skd->ksd', vin[slot])
        for copy in put(b, slot):
            copy.start()

        @pl.when(b + depth_in < steps)
        def _():
            for copy in bring(b + depth_in, slot):
                copy.start()
        return 0

    done = [0]

    def fill(n):
        n = min(n, steps - done[0])
        if n > 0:
            lax.fori_loop(done[0], done[0] + n, turn, 0)
            done[0] += n

    for b in range(depth_in):
        for copy in bring(b, b):
            copy.start()
    packs[p.b, p.j] = pack_ref[...]
    csa[p.j] = cs_ref[...]

    meet(p.mates() + [t.mate(da, other) for da in range(1, side) for other in (False, True)])

    gather = ColumnGather(p, sends, wq, (s_up, r_up), (s_dn, r_dn), (s_far, r_far))
    count = r_plus.shape[0]
    cut = xa.shape[1] // count
    tokens = RowGather(p, sends, lambda spot, k: xa.at[spot, pl.ds(k * cut, cut)], count,
                       (s_plus, r_plus), (s_minus, r_minus), (s_rfar, r_rfar), (s_pair, r_pair))
    landed(wq.at[p.b, p.j], s_wl.at[0])
    gather.own(0)
    for k, at in enumerate(rel):
        sends(pack_ref, packs.at[p.b, p.j], s_pk.at[k], r_pk.at[k], p.mate(*at))
    for k, at in enumerate(rel):
        landed(wl.at[k], s_wl.at[k + 1])
        sends(wl.at[k], wq.at[p.b, p.j], s_a2a.at[k], r_a2a.at[k], p.mate(*at))
    for k, at in enumerate(rel):
        sends(cs_ref, csa.at[p.j], s_cs.at[k], r_cs.at[k], p.mate(*at))
    landed(xa.at[p.j], s_loc.at[0])
    for k in range(count):
        tokens.own(k)

    for k in range(row - 1):
        landed(packs.at[p.b, p.spot(*rel[k])], r_pk.at[mirror(rel, k, side)])
    pv = packs.at[p.b]
    sends(pv, pv, s_pv.at[0], r_pv.at[0], p.above(1))
    sends(pv, pv, s_pv.at[1], r_pv.at[1], p.above(back))
    for k in range(row - 1):
        landed(wq.at[p.b, p.spot(*rel[k])], r_a2a.at[mirror(rel, k, side)])
        gather.own(k + 1)
        fill(2)
    pu = packs.at[p.line(back)]
    landed(pu, r_pv.at[0])
    sends(pu, pu, s_pv.at[2], r_pv.at[2], p.above(1))
    landed(packs.at[p.line(1)], r_pv.at[1])
    landed(packs.at[p.line(2)], r_pv.at[2])
    for k in range(row - 1):
        landed(csa.at[p.spot(*rel[k])], r_cs.at[mirror(rel, k, side)])
    out_pack = pltpu.make_async_copy(packs, pack_out, s_loc.at[2])
    out_pack.start()

    model = xa.shape[-1]

    def norm(spot):
        total = jnp.zeros((xa.shape[1], head), F32)
        for i in range(model // head):
            v = xa[spot, :, i * head:(i + 1) * head].astype(F32)
            total = total + v * v
        inv = lax.rsqrt(jnp.sum(total, axis=-1, keepdims=True) / model + NORM_EPS)
        for i in range(model // head):
            v = xa[spot, :, i * head:(i + 1) * head].astype(F32)
            g = packs[i // row, i % row, 0:1, :]
            hh[spot, :, i * head:(i + 1) * head] = (v * inv * g).astype(BF16)

    span = row * depth

    def part(da, db):
        chip = lax.rem(p.a + da, side)
        rows = hh[pl.ds(chip * CORES, CORES), :, pl.ds(pl.multiple_of(p.line(db) * span, span), span)]
        rows = rows.reshape(CORES * hh.shape[1], span)
        return jnp.dot(rows, wq[p.line(db)].reshape(span, wide), preferred_element_type=F32)

    def bias(m):
        e, k = m // 3, lax.rem(m, 3)
        out = 0.0
        for c in range(CORES):
            d = e * CORES + c
            out = out + packs[d // row, lax.rem(d, row), pl.ds(3 + k, 1), :]
        return out

    lanes = lax.broadcasted_iota(jnp.int32, (1, head), 1)

    def finish(da):
        total = acc[da] + part(da, 2)
        chip = lax.rem(p.a + da, side)
        cs = csa[pl.ds(chip * CORES, CORES)].reshape(CORES * csa.shape[1], head)
        turned = pltpu.roll(cs, head // 2, 1)
        low = lanes < head // 2
        cos = jnp.where(low, cs, turned)
        sin = jnp.where(low, -turned, cs)
        n_q = heads // kv
        for i in range(n_q + 2):
            m = p.j * n_q + i if i < n_q else (heads + p.j if i == n_q else heads + kv + p.j)
            v = total[:, i * head:(i + 1) * head] + bias(m)
            if i <= n_q:
                v = v * cos + pltpu.roll(v, head // 2, 1) * sin
            res[da * CORES:(da + 1) * CORES, :, i * head:(i + 1) * head] = v.astype(BF16).reshape(CORES, -1, head)
        for c in range(CORES):
            src = res.at[da * CORES + c]
            if da:
                sends(src, qkv_out.at[p.j], s_res.at[da * CORES + c], r_res.at[p.j], p.device(chip, p.b, c))
            else:
                @pl.when(p.c == c)
                def _():
                    pltpu.make_async_copy(src, qkv_out.at[p.j], r_res.at[p.j]).start()

                @pl.when(p.c != c)
                def _():
                    pltpu.make_async_remote_copy(
                        src_ref=src, dst_ref=qkv_out.at[p.j], send_sem=s_res.at[0], recv_sem=r_res.at[p.j],
                        device_id={AXIS: p.device(chip, p.b, c)}, device_id_type=MESH_ID).start()

    norm(p.spot(0))
    tokens.from_pair(0)
    norm(p.spot(0, True))
    for k in range(0, 4):
        gather.near(k)
        fill(2)
    acc[0] = part(0, 0)
    for k in range(count):
        if k % 2 == 0:
            for i in range(4 + k, 4 + k + 2):
                gather.near(i)
            fill(2)
        tokens.near(k)
        fill(2)
    for k, at in enumerate(rel):
        landed(wol.at[k], s_wol.at[k])
        sends(wol.at[k], wo_out.at[t.j], s_o.at[k], r_o.at[k], t.mate(*at))
    for k, at in enumerate(rel):
        src = xa.at[p.j, :, pl.ds(pl.multiple_of(t.spot(*at) * ow, head), ow)]
        sends(src, xb_out.at[t.j], s_x.at[k], r_x.at[k], t.mate(*at))
    landed(wol.at[row - 1], s_wol.at[row - 1])
    own_o = pltpu.make_async_copy(wol.at[row - 1], wo_out.at[t.j], s_loc.at[1])
    own_o.start()
    own_x = pltpu.make_async_copy(xa.at[p.j, :, pl.ds(pl.multiple_of(t.j * ow, head), ow)], xb_out.at[t.j], s_loc.at[3])
    own_x.start()
    fill(steps)
    acc[0] += part(0, 1)
    acc[0] += part(0, back)
    for da in (back, 1):
        norm(p.spot(da))
        tokens.from_pair(da)
        norm(p.spot(da, True))
        acc[da] = part(da, 0)
        acc[da] += part(da, 1)
        acc[da] += part(da, back)
    for k in range(count):
        tokens.far(k)
    norm(p.spot(2))
    tokens.from_pair(2)
    norm(p.spot(2, True))
    for k in range(row):
        gather.far(k)
    finish(1)
    finish(back)
    acc[2] = part(2, 0)
    acc[2] += part(2, 1)
    acc[2] += part(2, back)
    finish(2)
    finish(0)
    for k in range(row - 1):
        landed(wo_out.at[t.spot(*rel[k])], r_o.at[mirror(rel, k, side)])
        landed(xb_out.at[t.spot(*rel[k])], r_x.at[mirror(rel, k, side)])
    for b in range(steps - depth_in, steps):
        for copy in put(b, b % depth_in):
            copy.wait()
    for i in range(row):
        landed(qkv_out.at[i], r_res.at[i])
    own_o.wait()
    own_x.wait()
    out_pack.wait()
    landed(res.at[0], s_res.at[0])
    sends.finish()


def output_kernel(side, kv, experts, len_ref, sink_ref, qkv_ref, kt_ref, vt_ref, wo_ref, xb_ref, packs, br_ref,
                  resid_out, logit_out,
                  kb0, kb1, vb0, vb1, sb0, sb1, mb0, mb1, lb0, lb1, oa, wq, xbv, acc, res, own,
                  s_k, s_v, s_loc, s_plus, r_plus, s_minus, r_minus, s_rfar, r_rfar, s_pair, r_pair,
                  s_up, r_up, s_dn, r_dn, s_far, r_far, s_res, r_res):
    p = Place(side, across=True)
    row = p.row
    back = side - 1
    head = packs.shape[-1]
    depth = wq.shape[2]
    wide = wq.shape[3]
    n_tok = oa.shape[1]
    n_req = kt_ref.shape[0]
    slots = kt_ref.shape[2]
    new = n_tok // n_req
    group = qkv_ref.shape[2] // head - 2
    rows = group * new
    total = n_req * kv
    scale = head ** -0.5 * LOG2E
    block = min(512, slots)
    sends = Sends()
    loads = [pltpu.make_async_copy(wo_ref, wq.at[p.b], s_loc.at[0]),
             pltpu.make_async_copy(xb_ref, xbv, s_loc.at[1])]
    for copy in loads:
        copy.start()

    def fetch(n, which, buf, sem):
        n = jnp.minimum(n, total - 1)
        return pltpu.make_async_copy(which.at[n // kv, lax.rem(n, kv)], buf, sem)

    fetch(0, kt_ref, kb0, s_k.at[0]).start()
    fetch(0, vt_ref, vb0, s_v.at[0]).start()
    fetch(1, kt_ref, kb1, s_k.at[1]).start()
    fetch(1, vt_ref, vb1, s_v.at[1]).start()
    meet(p.mates() + [p.above(1), p.above(back)])
    gather = ColumnGather(p, sends, wq, (s_up, r_up), (s_dn, r_dn), (s_far, r_far))
    lanes = row * wide // 2
    tokens = RowGather(
        p, sends, lambda spot, k: oa.at[spot, pl.ds(k // 2 * new, new), pl.ds(k % 2 * lanes, lanes)], 2 * n_req,
        (s_plus, r_plus), (s_minus, r_minus), (s_rfar, r_rfar), (s_pair, r_pair))
    count = tokens.count
    loads[0].wait()
    for k in range(row):
        gather.own(k)
    loads[1].wait()

    def place(r):
        return pl.ds(pl.multiple_of(r * new, new), new)

    ri = lax.rem(lax.broadcasted_iota(jnp.int32, (rows, head), 0), new)
    ci = lax.broadcasted_iota(jnp.int32, (rows, head), 1)

    def first(n, sb, mb, lb, kb):
        n = jnp.minimum(n, total - 1)
        r, i = n // kv, lax.rem(n, kv)
        q = jnp.concatenate([qkv_ref[i, place(r), g * head:(g + 1) * head] for g in range(group)], axis=0)
        length = len_ref[r]
        kn = qkv_ref[i, place(r), group * head:(group + 1) * head]
        kn = jnp.concatenate([kn, jnp.zeros((head - new, head), BF16)], axis=0)
        s = jnp.where(ri >= ci, dot_nt(q, kn), -1e30)
        sb[:, slots:] = s
        m = s
        for b in range(slots // block):
            s = dot_nt(q, kb[b * block:(b + 1) * block])
            s = jnp.where(b * block + lax.broadcasted_iota(jnp.int32, (1, block), 1) < length, s, -1e30)
            sb[:, b * block:(b + 1) * block] = s
            for k in range(block // head):
                m = jnp.maximum(m, s[:, k * head:(k + 1) * head])
            yield
        m = jnp.max(m, axis=-1, keepdims=True) * scale
        sink = jnp.concatenate([jnp.full((new, head), sink_ref[i * group + g] * LOG2E, F32) for g in range(group)], axis=0)
        m = jnp.maximum(m, sink)
        mb[...] = m
        lb[...] = jnp.exp2(sink - m)

    def second(n, sb, mb, lb, vb):
        r, i = n // kv, lax.rem(n, kv)
        m = mb[...]
        vn = qkv_ref[i, place(r), (group + 1) * head:]
        vn = jnp.concatenate([vn, jnp.zeros((head - new, head), BF16)], axis=0)
        pr = jnp.exp2(sb[:, slots:] * scale - m)
        low = pr
        out = jnp.dot(pr.astype(BF16), vn, preferred_element_type=F32)
        for b in range(slots // block):
            prs = []
            for k in range(block // head):
                at = b * block + k * head
                pr = jnp.exp2(sb[:, at:at + head] * scale - m)
                low = low + pr
                prs.append(pr.astype(BF16))
            out = out + jnp.dot(jnp.concatenate(prs, axis=1), vb[b * block:(b + 1) * block], preferred_element_type=F32)
            yield
        out = (out / (jnp.sum(low, axis=-1, keepdims=True) + lb[...])).astype(BF16)
        for g in range(group):
            at = pl.multiple_of((i * group + g) * head, head)
            oa[p.j, place(r), pl.ds(at, head)] = out[g * new:(g + 1) * new]

    def run(*work):
        work = list(work)
        while work:
            for w in list(work):
                if next(w, w) is w:
                    work.remove(w)

    fetch(0, kt_ref, kb0, s_k.at[0]).wait()
    run(first(0, sb0, mb0, lb0, kb0))
    fetch(2, kt_ref, kb0, s_k.at[0]).start()
    turns = total // 2
    each = turns // count

    def events(h):
        out = []
        if (h + 1) % each == 0:
            out.append((tokens.own, h // each))
        for k in range(count):
            if h == (k + 2) * each:
                out.append((tokens.near, k))
            if h == (k + 3) * each + each // 2:
                out.append((tokens.far, k))
        if h >= turns // 2:
            for k in range(row):
                if turns // 2 + k // 2 == h:
                    out.append((gather.near, k))
        return out

    def body(h, _):
        n = 2 * h
        fetch(n, vt_ref, vb0, s_v.at[0]).wait()
        fetch(n + 1, kt_ref, kb1, s_k.at[1]).wait()
        run(first(n + 1, sb1, mb1, lb1, kb1), second(n, sb0, mb0, lb0, vb0))
        fetch(n + 2, vt_ref, vb0, s_v.at[0]).start()
        fetch(n + 3, kt_ref, kb1, s_k.at[1]).start()
        fetch(n + 1, vt_ref, vb1, s_v.at[1]).wait()
        fetch(n + 2, kt_ref, kb0, s_k.at[0]).wait()
        run(first(n + 2, sb0, mb0, lb0, kb0), second(n + 1, sb1, mb1, lb1, vb1))
        fetch(n + 3, vt_ref, vb1, s_v.at[1]).start()
        fetch(n + 4, kt_ref, kb0, s_k.at[0]).start()
        for at in range(turns):
            todo = events(at)
            if todo:
                @pl.when(h == at)
                def _():
                    for act, k in todo:
                        act(k)
        return 0

    lax.fori_loop(0, turns, body, 0)
    for which, buf, sem in ((vt_ref, vb0, s_v.at[0]), (vt_ref, vb1, s_v.at[1]), (kt_ref, kb0, s_k.at[0]), (kt_ref, kb1, s_k.at[1])):
        fetch(0, which, buf, sem).wait()
    past = [e for h in range(turns) for e in events(h)]

    def rest(act, k):
        if not any(a == act and i == k for a, i in past):
            act(k)

    def part(da, db):
        chip = lax.rem(p.a + da, side)
        cols = [oa[pl.ds(chip * CORES, CORES), :, pl.ds(pl.multiple_of(p.device(a, p.line(db), 0) * depth, depth), CORES * depth)]
                for a in range(side)]
        lhs = jnp.concatenate([v.reshape(CORES * n_tok, CORES * depth) for v in cols], axis=-1)
        return jnp.dot(lhs, wq[p.line(db)].reshape(row * depth, wide), preferred_element_type=F32)

    def finish(da):
        total = acc[da] + part(da, 2)
        chip = lax.rem(p.a + da, side)
        for i in range(wide // head):
            d = p.j * (wide // head) + i
            b = packs[d // row, lax.rem(d, row), 1:2, :]
            at = pl.ds(i * head, head)
            base = xbv[pl.ds(chip * CORES, CORES), :, at].reshape(-1, head).astype(F32)
            v = base + (total[:, i * head:(i + 1) * head] + b)
            res[da * CORES:(da + 1) * CORES, :, at] = v.astype(BF16).reshape(CORES, -1, head)
        for c in range(CORES):
            src = res.at[da * CORES + c]
            if da:
                sends(src, own.at[p.j], s_res.at[da * CORES + c], r_res.at[p.j], p.device(chip, p.b, c))
            else:
                @pl.when(p.c == c)
                def _():
                    own[p.j] = src[...]

                @pl.when(p.c != c)
                def _():
                    pltpu.make_async_remote_copy(
                        src_ref=src, dst_ref=own.at[p.j], send_sem=s_res.at[0], recv_sem=r_res.at[p.j],
                        device_id={AXIS: p.device(chip, p.b, c)}, device_id_type=MESH_ID).start()

    for k in range(row):
        rest(gather.near, k)
    for k in range(count):
        rest(tokens.near, k)
        if k:
            rest(tokens.far, k - 1)
    tokens.from_pair(0)
    acc[0] = part(0, 0)
    acc[0] += part(0, 1)
    acc[0] += part(0, back)
    for da in (back, 1):
        tokens.from_pair(da)
        acc[da] = part(da, 0)
        acc[da] += part(da, 1)
        acc[da] += part(da, back)
    rest(tokens.far, count - 1)
    for k in range(row):
        gather.far(k)
    finish(1)
    finish(back)
    tokens.from_pair(2)
    acc[2] = part(2, 0)
    acc[2] += part(2, 1)
    acc[2] += part(2, back)
    finish(2)
    finish(0)
    for da, other in rel_order(side):
        spot = p.spot(da, other)
        landed(own.at[spot], r_res.at[spot])
    model = row * wide
    outs = []
    for i in range(row):
        copy = pltpu.make_async_copy(own.at[i], resid_out.at[:, pl.ds(i * wide, wide)], s_loc.at[3 + i])
        copy.start()
        outs.append(copy)
    square = jnp.zeros((n_tok, head), F32)
    for i in range(row):
        for k in range(wide // head):
            v = own[i, :, k * head:(k + 1) * head].astype(F32)
            square = square + v * v
    inv = lax.rsqrt(jnp.sum(square, axis=-1, keepdims=True) / model + NORM_EPS)
    logits = jnp.zeros((n_tok, experts), F32)
    for i in range(row):
        for k in range(wide // head):
            d = i * (wide // head) + k
            v = own[i, :, k * head:(k + 1) * head].astype(F32)
            g = (v * inv * packs[d // row, d % row, 2:3, :]).astype(BF16)
            w = packs[d // row, d % row, 8:8 + experts, :].astype(BF16)
            logits = logits + dot_nt(g, w)
    logit_out[...] = logits + br_ref[...]
    for copy in outs:
        copy.wait()
    landed(res.at[0], s_res.at[0])
    sends.finish()


def dma(*shape):
    return pltpu.SemaphoreType.DMA(shape)


def solution(mesh):
    row_spec = P(('dp', 'fsdp'))
    shard_spec = P('fsdp')
    whole_spec = P()
    n_dev = mesh.shape[AXIS]
    side = math.isqrt(n_dev // CORES)
    row = side * CORES
    hbm = pl.BlockSpec(memory_space=pl.ANY)
    vmem = pl.BlockSpec(memory_space=pltpu.VMEM)
    smem = pl.BlockSpec(memory_space=pltpu.SMEM)

    def local_step(tokens, k_cache, v_cache, prefix_len, rope_cos, rope_sin, norm_attn, w_qkv, b_qkv, sink_logits, w_out, b_out, norm_router, w_router, b_router):
        n_req, n_new, model = tokens.shape
        kv, head = k_cache.shape[2:]
        heads = sink_logits.shape[0]
        experts = b_router.shape[0]
        depth = w_qkv.shape[0]
        n_tok = n_req * n_new
        wide = w_qkv.shape[1] // row
        ow = model // row
        flat = tokens.reshape(n_tok, model)
        cs = jnp.concatenate([rope_cos, rope_sin], axis=-1).reshape(n_tok, head)
        core = lax.rem(lax.axis_index(AXIS), CORES)
        bias_pad = lax.dynamic_update_slice(jnp.zeros((3 * head,), F32), b_qkv.astype(F32), (core * b_qkv.shape[0],))
        pack = jnp.concatenate([
            norm_attn.astype(F32)[None], b_out.astype(F32)[None], norm_router.astype(F32)[None],
            bias_pad.reshape(3, head), jnp.zeros((2, head), F32), w_router.astype(F32).T], axis=0)
        n_pack = pack.shape[0]

        pieces = 4
        turn = 256
        slots = k_cache.shape[1]
        qkv, xb, packs, wo, kt, vt = pl.pallas_call(
            functools.partial(project_kernel, side, heads, kv),
            out_shape=(jax.ShapeDtypeStruct((row, n_tok, wide), BF16),
                       jax.ShapeDtypeStruct((row, n_tok, ow), BF16),
                       jax.ShapeDtypeStruct((side, row, n_pack, head), F32),
                       jax.ShapeDtypeStruct((row, depth, ow), BF16),
                       jax.ShapeDtypeStruct((n_req, kv, slots, head), BF16),
                       jax.ShapeDtypeStruct((n_req, kv, slots, head), BF16)),
            in_specs=[hbm, hbm, hbm, vmem, vmem, hbm, hbm],
            out_specs=(hbm,) * 6,
            scratch_shapes=[
                pltpu.VMEM((row - 1, depth, wide), BF16),
                pltpu.VMEM((row, depth, ow), BF16),
                pltpu.VMEM((side, row, depth, wide), BF16),
                pltpu.VMEM((row, n_tok, model), BF16),
                pltpu.VMEM((row, n_tok, model), BF16),
                pltpu.VMEM((row, n_tok, head), F32),
                pltpu.VMEM((side, row, n_pack, head), F32),
                pltpu.VMEM((side, CORES * n_tok, wide), F32),
                pltpu.VMEM((row, n_tok, wide), BF16),
                pltpu.VMEM((4, turn, kv, head), BF16), pltpu.VMEM((4, turn, kv, head), BF16),
                pltpu.VMEM((4, kv, turn, head), BF16), pltpu.VMEM((4, kv, turn, head), BF16),
                dma(row), dma(row), dma(4), dma(row), dma(row), dma(row), dma(row), dma(row), dma(row),
                dma(row), dma(row), dma(row), dma(row), dma(3), dma(3),
                dma(pieces), dma(pieces), dma(pieces), dma(pieces), dma(pieces), dma(pieces), dma(4 * pieces), dma(4 * pieces),
                dma(row), dma(row), dma(row), dma(row), dma(row), dma(row), dma(row), dma(row), dma(8), dma(8)],
            compiler_params=pltpu.CompilerParams(collective_id=0, has_side_effects=True, vmem_limit_bytes=60 * 2**20),
            name='project',
        )(w_qkv, w_out, flat, cs, pack, k_cache, v_cache)

        n_row = heads // kv * n_new
        resid, logits = pl.pallas_call(
            functools.partial(output_kernel, side, kv, experts),
            out_shape=(jax.ShapeDtypeStruct((n_tok, model), BF16), jax.ShapeDtypeStruct((n_tok, experts), F32)),
            in_specs=[smem, smem, vmem, hbm, hbm, hbm, hbm, vmem, vmem],
            out_specs=(hbm, vmem),
            scratch_shapes=[
                pltpu.VMEM((slots, head), BF16), pltpu.VMEM((slots, head), BF16),
                pltpu.VMEM((slots, head), BF16), pltpu.VMEM((slots, head), BF16),
                pltpu.VMEM((n_row, slots + head), F32), pltpu.VMEM((n_row, slots + head), F32),
                pltpu.VMEM((n_row, head), F32), pltpu.VMEM((n_row, head), F32),
                pltpu.VMEM((n_row, head), F32), pltpu.VMEM((n_row, head), F32),
                pltpu.VMEM((row, n_tok, model), BF16),
                pltpu.VMEM((side, row, depth, ow), BF16),
                pltpu.VMEM((row, n_tok, ow), BF16),
                pltpu.VMEM((side, CORES * n_tok, ow), F32),
                pltpu.VMEM((row, n_tok, ow), BF16),
                pltpu.VMEM((row, n_tok, ow), BF16),
                dma(2), dma(2), dma(3 + row),
                dma(pieces), dma(pieces), dma(pieces), dma(pieces), dma(pieces), dma(pieces), dma(4 * pieces), dma(4 * pieces),
                dma(row), dma(row), dma(row), dma(row), dma(row), dma(row), dma(row), dma(row)],
            compiler_params=pltpu.CompilerParams(collective_id=1, has_side_effects=True, vmem_limit_bytes=56 * 2**20),
            name='output',
        )(prefix_len, sink_logits, qkv, kt, vt, wo, xb, packs, b_router.reshape(1, experts))

        split = qkv.reshape(row, n_req, n_new, wide)
        gw = wide - 2 * head
        k_new = jnp.transpose(split[..., gw:gw + head], (1, 2, 0, 3))
        v_new = jnp.transpose(split[..., gw + head:], (1, 2, 0, 3))
        return (resid.reshape(n_req, n_new, model), logits.reshape(n_req, n_new, experts), k_new, v_new)

    in_specs = (row_spec, row_spec, row_spec, row_spec, row_spec, row_spec, shard_spec, shard_spec, shard_spec, whole_spec, shard_spec, shard_spec, shard_spec, shard_spec, whole_spec)
    out_specs = (row_spec, row_spec, row_spec, row_spec)
    return jax.shard_map(local_step, mesh=mesh, in_specs=in_specs, out_specs=out_specs, check_vma=False)
```

time: 243 us -> 174 us (0.72)
  Pallas kernels: 232 us -> 161 us
    pallas_call x2 -> x1, Pallas kernels: 130 us -> 66 us  [local_step(): pl.pallas_call(functools.partial(output_kernel, side, kv, experts), out_s...]
    pallas_call x1, Pallas kernels: 102 us -> 94.8 us  [local_step(): pl.pallas_call(functools.partial(project_kernel, side, heads, kv), out_sh...]
    unnamed x18 -> x4, local copies, waits for them, and re-layouts: 3.43 us -> 5.55 us
where the time goes in v2:
time: 174 us
  Pallas kernels  161 us (93%)
  local copies, waits for them, and re-layouts  7.82 us (4%)
  other arithmetic  4.34 us (2%)
    pallas_call x1, Pallas kernels, local_step(): pl.pallas_call(functools.partial(project_kernel, side, heads, kv), out_sh...  94.8 us
    pallas_call x1, Pallas kernels, local_step(): pl.pallas_call(functools.partial(output_kernel, side, kv, experts), out_s...  66 us
    unnamed x4, local copies, waits for them, and re-layouts  5.55 us

profile of v2, /device:TPU:97, one launch (start us, length us, event | category | flops | bytes accessed | tf_op | source)
XLA Modules:
  0.0 173.6 jit_solution(10343879314344450836)
XLA Ops:
  0.6 0.7 bitcast_convert_fusion.2
  1.3 0.7 bitcast_convert_fusion
  2.0 0.7 convert_dynamic-update-slice_fusion
  2.7 0.7 convert_bitcast_fusion
  3.4 1.2 concatenate.7.pack_ref
  4.6 1.6 pad_maximum_fusion
  6.2 94.8 %project.1 = (bf16[8,128,768]{2,1,0:T(8,128)(2,1)}, bf16[8,128,512]{2,1,0:T(8,128)(2,1)}, f32[4,8,16,128]{3,2,1,0:T(8,128)}, bf16[8,128,512]{2,1,0:T(8,128)(2,1)...) custom-call(bf16[128,6144]{1,0:T(8,128)(2,1)} %w_ref.1, bf16[128,4096]{1,0:T(8,128)(2,1)} %wo_ref.1, ...), custom_call_target="tpu_custom_call" | custom-call | tf_op jit(solution)/shard_map/project/pallas_call | solution.py:680
  101.0 66.0 %output.1 = (bf16[128,4096]{1,0:T(8,128)(2,1)}, f32[128,8]{1,0:T(8,128)}) custom-call(s32[2]{0:T(128)} %len_ref.1, f32[32]{0:T(128)} %sink_ref.1, bf16[8,128,768]{2,1,0:T(8,128)(2,1)} %get-tuple-element.12.qkv_ref, bf16[2,8,4096,128]{3,2,1,0:T(8,128)(2,1)} %get-tuple-element.13.kt_ref, bf16[2,8,4096,128]{3,2,1,0:T(8,128)(2,1)} %get-tuple-element.14.vt_ref, ...), custom_call_target="tpu_custom_call" | custom-call | tf_op jit(solution)/shard_map/output/pallas_call | solution.py:711
  167.0 1.5 copy.21
  168.5 1.1 fusion
  169.6 0.9 copy.26
  170.5 0.9 copy.27
  171.3 2.3 %copy.30 = bf16[2,64,4096]{2,1,0:T(8,128)(2,1)} copy(bf16[2,64,4096]{2,1,0:T(8,128)(2,1)} %bitcast.26) | data formatting | bytes 2097152
  (2 shorter events, 0.0 us)

commit v3 on v2

--- a/solution.py
+++ b/solution.py
@@ -15,6 +15,8 @@
 BF16 = jnp.bfloat16
 F32 = jnp.float32
 LOG2E = 1.4426950408889634
+SAME, OTHER = False, True
+BOTH = (SAME, OTHER)
 
 
 class Place:
@@ -45,7 +47,7 @@
         return self.device(self.a, self.line(db), self.c)
 
     def mates(self):
-        return [self.mate(da, other) for da in range(self.side) for other in (False, True) if da or other]
+        return [self.mate(da, other) for da in range(self.side) for other in BOTH if da or other]
 
 
 class Sends:
@@ -75,12 +77,11 @@
 
 
 def rel_order(side):
-    return [(0, True), (1, False), (side - 1, False), (1, True), (side - 1, True), (2, False), (2, True)]
-
-
-def mirror(rel, k, side):
-    da, other = rel[k]
-    return rel.index(((side - da) % side, other))
+    return [(0, OTHER), (1, SAME), (side - 1, SAME), (1, OTHER), (side - 1, OTHER), (2, SAME), (2, OTHER)]
+
+
+def send_order(side):
+    return [(0, OTHER), (1, SAME), (side - 1, SAME), (2, SAME), (2, OTHER), (1, OTHER), (side - 1, OTHER)]
 
 
 class RowGather:
@@ -118,14 +119,14 @@
     def from_pair(self, da):
         group = {0: 0, self.p.side - 1: 1, 1: 2, 2: 3}[da]
         for k in range(self.count):
-            landed(self.view(self.p.spot(da, True), k), self.pair_sems[1].at[group * self.count + k])
+            landed(self.view(self.p.spot(da, OTHER), k), self.pair_sems[1].at[group * self.count + k])
 
 
 class ColumnGather:
     def __init__(self, place, sends, buf, up, down, far):
         self.p, self.sends, self.buf = place, sends, buf
         self.up, self.down, self.far_sems = up, down, far
-        self.order = [(0, False)] + rel_order(place.side)
+        self.order = [(0, SAME)] + rel_order(place.side)
 
     def go(self, line, k, sems, db):
         v = self.buf.at[line, self.p.spot(*self.order[k])]
@@ -149,16 +150,44 @@
         landed(self.buf.at[self.p.line(2), self.p.spot(*self.order[k])], self.far_sems[1].at[k])
 
 
+class Exchange:
+    def __init__(self, place, sends, src, dst, relay, sems, hand_sems):
+        self.p, self.sends, self.src, self.dst, self.relay = place, sends, src, dst, relay
+        (self.s, self.r), (self.hs, self.hr, self.fs) = sems, hand_sems
+
+    def send(self, da, other):
+        p, slot = self.p, da * CORES + other
+        if da == 2:
+            way = p.side - 1 if other else 1
+            self.sends(self.src(da, other), self.relay.at[int(other)], self.hs.at[int(other)], self.hr.at[int(other)],
+                       p.mate(way))
+        else:
+            self.sends(self.src(da, other), self.dst(p.j), self.s.at[slot], self.r.at[p.j], p.mate(da, other))
+
+    def hand(self):
+        p, back = self.p, self.p.side - 1
+        for lane, origin, way in ((0, p.spot(back), p.mate(1)), (1, p.spot(1), p.mate(back, OTHER))):
+            landed(self.relay.at[lane], self.hr.at[lane])
+            self.sends(self.relay.at[lane], self.dst(origin), self.fs.at[lane], self.r.at[origin], way)
+
+    def arrived(self, da, other):
+        spot = self.p.spot(da, other)
+        landed(self.dst(spot), self.r.at[spot])
+
+
 def dot_nt(a, b):
     return lax.dot_general(a, b, (((1,), (1,)), ((), ())), preferred_element_type=F32)
 
 
-def project_kernel(side, heads, kv, w_ref, wo_ref, x_ref, cs_ref, pack_ref, k_ref, v_ref,
+def project_kernel(side, heads, kv, w_ref, wo_ref, x_ref, cos_ref, sin_ref, na_ref, bo_ref, nr_ref, bq_ref, wr_ref,
+                   k_ref, v_ref,
                    qkv_out, xb_out, pack_out, wo_out, kt_out, vt_out,
-                   wl, wol, wq, xa, hh, csa, packs, acc, res, kin, vin, kmid, vmid,
-                   s_wl, s_wol, s_loc, s_a2a, r_a2a, s_o, r_o, s_x, r_x, s_cs, r_cs, s_pk, r_pk, s_pv, r_pv,
+                   wl, wol, wq, xa, hh, csa, packs, acc, res, kin, vin, kmid, vmid, pass_w, pass_o, pass_x, pass_r,
+                   s_wl, s_wol, s_loc, s_a2a, r_a2a, s_o, r_o, s_x, r_x, s_pk, r_pk, s_pv, r_pv,
                    s_plus, r_plus, s_minus, r_minus, s_rfar, r_rfar, s_pair, r_pair,
-                   s_up, r_up, s_dn, r_dn, s_far, r_far, s_res, r_res, s_in, s_mid):
+                   c_plus, d_plus, c_minus, d_minus, c_far, d_far, c_pair, d_pair,
+                   s_up, r_up, s_dn, r_dn, s_far, r_far, s_res, r_res, s_in, s_mid,
+                   h_w, h_o, h_x, h_r):
     p = Place(side)
     t = Place(side, across=True)
     row = p.row
@@ -169,6 +198,7 @@
     wide = qw + 2 * head
     ow = wol.shape[-1]
     rel = rel_order(side)
+    order = send_order(side)
     sends = Sends()
 
     def take(spot, dst, sem):
@@ -182,7 +212,7 @@
     for k, at in enumerate(rel):
         take(p.spot(*at), wl.at[k], s_wl.at[k + 1])
     pltpu.make_async_copy(x_ref, xa.at[p.j], s_loc.at[0]).start()
-    for k, at in enumerate(rel + [(0, False)]):
+    for k, at in enumerate(rel + [(0, SAME)]):
         pltpu.make_async_copy(wo_ref.at[:, pl.ds(pl.multiple_of(t.spot(*at) * ow, head), ow)], wol.at[k],
                               s_wol.at[k]).start()
 
@@ -231,45 +261,66 @@
     for b in range(depth_in):
         for copy in bring(b, b):
             copy.start()
-    packs[p.b, p.j] = pack_ref[...]
-    csa[p.j] = cs_ref[...]
-
-    meet(p.mates() + [t.mate(da, other) for da in range(1, side) for other in (False, True)])
+    packs[p.b, p.j] = jnp.concatenate(
+        [na_ref[...].astype(F32), bo_ref[...].astype(F32), nr_ref[...].astype(F32), bq_ref[...],
+         jnp.zeros((2, head), F32), wr_ref[...].astype(F32)], axis=0)
+    csa[p.j] = jnp.concatenate([cos_ref[...], sin_ref[...]], axis=-1)
+
+    meet(p.mates() + [t.mate(da, other) for da in range(1, side) for other in BOTH])
 
     gather = ColumnGather(p, sends, wq, (s_up, r_up), (s_dn, r_dn), (s_far, r_far))
     count = r_plus.shape[0]
     cut = xa.shape[1] // count
     tokens = RowGather(p, sends, lambda spot, k: xa.at[spot, pl.ds(k * cut, cut)], count,
                        (s_plus, r_plus), (s_minus, r_minus), (s_rfar, r_rfar), (s_pair, r_pair))
+    turns = d_plus.shape[0]
+    cut_cs = csa.shape[1] // turns
+    tables = RowGather(p, sends, lambda spot, k: csa.at[spot, pl.ds(k * cut_cs, cut_cs)], turns,
+                       (c_plus, d_plus), (c_minus, d_minus), (c_far, d_far), (c_pair, d_pair))
+    swap_w = Exchange(p, sends, lambda da, other: wl.at[rel.index((da, other))], lambda spot: wq.at[p.b, spot], pass_w,
+                      (s_a2a, r_a2a), (h_w.at[0], h_w.at[1], h_w.at[2]))
+    swap_o = Exchange(t, sends, lambda da, other: wol.at[rel.index((da, other))], lambda spot: wo_out.at[spot], pass_o,
+                      (s_o, r_o), (h_o.at[0], h_o.at[1], h_o.at[2]))
+    swap_x = Exchange(
+        t, sends, lambda da, other: xa.at[p.j, :, pl.ds(pl.multiple_of(t.spot(da, other) * ow, head), ow)],
+        lambda spot: xb_out.at[spot], pass_x, (s_x, r_x), (h_x.at[0], h_x.at[1], h_x.at[2]))
+    swap_r = Exchange(
+        p, sends, lambda da, other: res.at[da * CORES + (1 - p.c if other else p.c)],
+        lambda spot: qkv_out.at[spot], pass_r, (s_res, r_res), (h_r.at[0], h_r.at[1], h_r.at[2]))
     landed(wq.at[p.b, p.j], s_wl.at[0])
     gather.own(0)
+    mine = packs.at[p.b, p.j]
     for k, at in enumerate(rel):
-        sends(pack_ref, packs.at[p.b, p.j], s_pk.at[k], r_pk.at[k], p.mate(*at))
-    for k, at in enumerate(rel):
-        landed(wl.at[k], s_wl.at[k + 1])
-        sends(wl.at[k], wq.at[p.b, p.j], s_a2a.at[k], r_a2a.at[k], p.mate(*at))
-    for k, at in enumerate(rel):
-        sends(cs_ref, csa.at[p.j], s_cs.at[k], r_cs.at[k], p.mate(*at))
+        sends(mine, mine, s_pk.at[k], r_pk.at[p.j], p.mate(*at))
+    for at in order:
+        landed(wl.at[rel.index(at)], s_wl.at[rel.index(at) + 1])
+        swap_w.send(*at)
+    for k in range(turns):
+        tables.own(k)
     landed(xa.at[p.j], s_loc.at[0])
-    for k in range(count):
-        tokens.own(k)
-
-    for k in range(row - 1):
-        landed(packs.at[p.b, p.spot(*rel[k])], r_pk.at[mirror(rel, k, side)])
+    tokens.own(0)
+
+    for at in rel:
+        landed(packs.at[p.b, p.spot(*at)], r_pk.at[p.spot(*at)])
     pv = packs.at[p.b]
     sends(pv, pv, s_pv.at[0], r_pv.at[0], p.above(1))
     sends(pv, pv, s_pv.at[1], r_pv.at[1], p.above(back))
-    for k in range(row - 1):
-        landed(wq.at[p.b, p.spot(*rel[k])], r_a2a.at[mirror(rel, k, side)])
+    for k, at in enumerate(rel):
+        swap_w.arrived(*at)
         gather.own(k + 1)
+        if k == 0:
+            pu = packs.at[p.line(back)]
+            landed(pu, r_pv.at[0])
+            sends(pu, pu, s_pv.at[2], r_pv.at[2], p.above(1))
+        if k == 2:
+            swap_w.hand()
+            for i in range(1, count):
+                tokens.own(i)
         fill(2)
-    pu = packs.at[p.line(back)]
-    landed(pu, r_pv.at[0])
-    sends(pu, pu, s_pv.at[2], r_pv.at[2], p.above(1))
     landed(packs.at[p.line(1)], r_pv.at[1])
     landed(packs.at[p.line(2)], r_pv.at[2])
-    for k in range(row - 1):
-        landed(csa.at[p.spot(*rel[k])], r_cs.at[mirror(rel, k, side)])
+    for k in range(turns):
+        tables.near(k)
     out_pack = pltpu.make_async_copy(packs, pack_out, s_loc.at[2])
     out_pack.start()
 
@@ -319,24 +370,15 @@
             if i <= n_q:
                 v = v * cos + pltpu.roll(v, head // 2, 1) * sin
             res[da * CORES:(da + 1) * CORES, :, i * head:(i + 1) * head] = v.astype(BF16).reshape(CORES, -1, head)
-        for c in range(CORES):
-            src = res.at[da * CORES + c]
-            if da:
-                sends(src, qkv_out.at[p.j], s_res.at[da * CORES + c], r_res.at[p.j], p.device(chip, p.b, c))
-            else:
-                @pl.when(p.c == c)
-                def _():
-                    pltpu.make_async_copy(src, qkv_out.at[p.j], r_res.at[p.j]).start()
-
-                @pl.when(p.c != c)
-                def _():
-                    pltpu.make_async_remote_copy(
-                        src_ref=src, dst_ref=qkv_out.at[p.j], send_sem=s_res.at[0], recv_sem=r_res.at[p.j],
-                        device_id={AXIS: p.device(chip, p.b, c)}, device_id_type=MESH_ID).start()
+        for other in BOTH:
+            if da or other:
+                swap_r.send(da, other)
+        if not da:
+            pltpu.make_async_copy(res.at[p.c], qkv_out.at[p.j], r_res.at[p.j]).start()
 
     norm(p.spot(0))
     tokens.from_pair(0)
-    norm(p.spot(0, True))
+    norm(p.spot(0, OTHER))
     for k in range(0, 4):
         gather.near(k)
         fill(2)
@@ -348,12 +390,13 @@
             fill(2)
         tokens.near(k)
         fill(2)
-    for k, at in enumerate(rel):
-        landed(wol.at[k], s_wol.at[k])
-        sends(wol.at[k], wo_out.at[t.j], s_o.at[k], r_o.at[k], t.mate(*at))
-    for k, at in enumerate(rel):
-        src = xa.at[p.j, :, pl.ds(pl.multiple_of(t.spot(*at) * ow, head), ow)]
-        sends(src, xb_out.at[t.j], s_x.at[k], r_x.at[k], t.mate(*at))
+    for at in order:
+        landed(wol.at[rel.index(at)], s_wol.at[rel.index(at)])
+        swap_o.send(*at)
+    for at in order:
+        swap_x.send(*at)
+    for k in range(turns):
+        tables.far(k)
     landed(wol.at[row - 1], s_wol.at[row - 1])
     own_o = pltpu.make_async_copy(wol.at[row - 1], wo_out.at[t.j], s_loc.at[1])
     own_o.start()
@@ -365,7 +408,7 @@
     for da in (back, 1):
         norm(p.spot(da))
         tokens.from_pair(da)
-        norm(p.spot(da, True))
+        norm(p.spot(da, OTHER))
         acc[da] = part(da, 0)
         acc[da] += part(da, 1)
         acc[da] += part(da, back)
@@ -373,19 +416,24 @@
         tokens.far(k)
     norm(p.spot(2))
     tokens.from_pair(2)
-    norm(p.spot(2, True))
-    for k in range(row):
-        gather.far(k)
-    finish(1)
-    finish(back)
+    norm(p.spot(2, OTHER))
+    for da in range(side):
+        tables.from_pair(da)
     acc[2] = part(2, 0)
     acc[2] += part(2, 1)
     acc[2] += part(2, back)
+    for k in range(row):
+        gather.far(k)
     finish(2)
+    finish(1)
+    finish(back)
+    swap_r.hand()
+    swap_o.hand()
     finish(0)
-    for k in range(row - 1):
-        landed(wo_out.at[t.spot(*rel[k])], r_o.at[mirror(rel, k, side)])
-        landed(xb_out.at[t.spot(*rel[k])], r_x.at[mirror(rel, k, side)])
+    swap_x.hand()
+    for at in rel:
+        swap_o.arrived(*at)
+        swap_x.arrived(*at)
     for b in range(steps - depth_in, steps):
         for copy in put(b, b % depth_in):
             copy.wait()
@@ -394,15 +442,13 @@
     own_o.wait()
     own_x.wait()
     out_pack.wait()
-    landed(res.at[0], s_res.at[0])
     sends.finish()
 
 
-def output_kernel(side, kv, experts, len_ref, sink_ref, qkv_ref, kt_ref, vt_ref, wo_ref, xb_ref, packs, br_ref,
-                  resid_out, logit_out,
-                  kb0, kb1, vb0, vb1, sb0, sb1, mb0, mb1, lb0, lb1, oa, wq, xbv, acc, res, own,
+def output_kernel(side, kv, len_ref, sink_ref, qkv_ref, kt_ref, vt_ref, wo_ref, xb_ref, packs, own,
+                  kb0, kb1, vb0, vb1, sb0, sb1, mb0, mb1, lb0, lb1, oa, wq, xbv, acc, res, pass_r,
                   s_k, s_v, s_loc, s_plus, r_plus, s_minus, r_minus, s_rfar, r_rfar, s_pair, r_pair,
-                  s_up, r_up, s_dn, r_dn, s_far, r_far, s_res, r_res):
+                  s_up, r_up, s_dn, r_dn, s_far, r_far, s_res, r_res, h_r):
     p = Place(side, across=True)
     row = p.row
     back = side - 1
@@ -434,11 +480,15 @@
     fetch(1, vt_ref, vb1, s_v.at[1]).start()
     meet(p.mates() + [p.above(1), p.above(back)])
     gather = ColumnGather(p, sends, wq, (s_up, r_up), (s_dn, r_dn), (s_far, r_far))
-    lanes = row * wide // 2
+    count = r_plus.shape[0]
+    cuts = count // n_req
+    lanes = row * wide // cuts
     tokens = RowGather(
-        p, sends, lambda spot, k: oa.at[spot, pl.ds(k // 2 * new, new), pl.ds(k % 2 * lanes, lanes)], 2 * n_req,
+        p, sends, lambda spot, k: oa.at[spot, pl.ds(k // cuts * new, new), pl.ds(k % cuts * lanes, lanes)], count,
         (s_plus, r_plus), (s_minus, r_minus), (s_rfar, r_rfar), (s_pair, r_pair))
-    count = tokens.count
+    swap_r = Exchange(
+        p, sends, lambda da, other: res.at[da * CORES + (1 - p.c if other else p.c)],
+        lambda spot: own.at[spot], pass_r, (s_res, r_res), (h_r.at[0], h_r.at[1], h_r.at[2]))
     loads[0].wait()
     for k in range(row):
         gather.own(k)
@@ -513,9 +563,9 @@
         if (h + 1) % each == 0:
             out.append((tokens.own, h // each))
         for k in range(count):
-            if h == (k + 2) * each:
+            if h == (k + 1) * each + 2:
                 out.append((tokens.near, k))
-            if h == (k + 3) * each + each // 2:
+            if h == (k + 1) * each + 4:
                 out.append((tokens.far, k))
         if h >= turns // 2:
             for k in range(row):
@@ -570,37 +620,24 @@
             base = xbv[pl.ds(chip * CORES, CORES), :, at].reshape(-1, head).astype(F32)
             v = base + (total[:, i * head:(i + 1) * head] + b)
             res[da * CORES:(da + 1) * CORES, :, at] = v.astype(BF16).reshape(CORES, -1, head)
-        for c in range(CORES):
-            src = res.at[da * CORES + c]
-            if da:
-                sends(src, own.at[p.j], s_res.at[da * CORES + c], r_res.at[p.j], p.device(chip, p.b, c))
-            else:
-                @pl.when(p.c == c)
-                def _():
-                    own[p.j] = src[...]
-
-                @pl.when(p.c != c)
-                def _():
-                    pltpu.make_async_remote_copy(
-                        src_ref=src, dst_ref=own.at[p.j], send_sem=s_res.at[0], recv_sem=r_res.at[p.j],
-                        device_id={AXIS: p.device(chip, p.b, c)}, device_id_type=MESH_ID).start()
+        for other in BOTH:
+            if da or other:
+                swap_r.send(da, other)
+        if not da:
+            pltpu.make_async_copy(res.at[p.c], own.at[p.j], r_res.at[p.j]).start()
 
     for k in range(row):
         rest(gather.near, k)
     for k in range(count):
         rest(tokens.near, k)
-        if k:
-            rest(tokens.far, k - 1)
-    tokens.from_pair(0)
-    acc[0] = part(0, 0)
-    acc[0] += part(0, 1)
-    acc[0] += part(0, back)
+        if k > 1:
+            rest(tokens.far, k - 2)
     for da in (back, 1):
         tokens.from_pair(da)
         acc[da] = part(da, 0)
         acc[da] += part(da, 1)
         acc[da] += part(da, back)
-    rest(tokens.far, count - 1)
+        rest(tokens.far, count - 2 if da == back else count - 1)
     for k in range(row):
         gather.far(k)
     finish(1)
@@ -610,35 +647,43 @@
     acc[2] += part(2, 1)
     acc[2] += part(2, back)
     finish(2)
+    tokens.from_pair(0)
+    acc[0] = part(0, 0)
+    acc[0] += part(0, 1)
+    acc[0] += part(0, back)
     finish(0)
-    for da, other in rel_order(side):
-        spot = p.spot(da, other)
-        landed(own.at[spot], r_res.at[spot])
+    swap_r.hand()
+    for i in range(row):
+        landed(own.at[i], r_res.at[i])
+    sends.finish()
+
+
+def close_kernel(own, qkv_ref, packs, br_ref, resid_out, logit_out, k_out, v_out):
+    row, n_tok, wide = own.shape
+    n_req, experts, new = logit_out.shape
+    head = packs.shape[-1]
     model = row * wide
-    outs = []
-    for i in range(row):
-        copy = pltpu.make_async_copy(own.at[i], resid_out.at[:, pl.ds(i * wide, wide)], s_loc.at[3 + i])
-        copy.start()
-        outs.append(copy)
+    for r in range(n_req):
+        k_out[r] = pltpu.einshape('jtd->tjd', qkv_ref[:, r * new:(r + 1) * new, :head])
+        v_out[r] = pltpu.einshape('jtd->tjd', qkv_ref[:, r * new:(r + 1) * new, head:])
     square = jnp.zeros((n_tok, head), F32)
     for i in range(row):
+        resid_out[:, i * wide:(i + 1) * wide] = own[i]
         for k in range(wide // head):
             v = own[i, :, k * head:(k + 1) * head].astype(F32)
             square = square + v * v
     inv = lax.rsqrt(jnp.sum(square, axis=-1, keepdims=True) / model + NORM_EPS)
-    logits = jnp.zeros((n_tok, experts), F32)
+    logits = jnp.zeros((experts, n_tok), F32)
     for i in range(row):
         for k in range(wide // head):
             d = i * (wide // head) + k
             v = own[i, :, k * head:(k + 1) * head].astype(F32)
             g = (v * inv * packs[d // row, d % row, 2:3, :]).astype(BF16)
             w = packs[d // row, d % row, 8:8 + experts, :].astype(BF16)
-            logits = logits + dot_nt(g, w)
-    logit_out[...] = logits + br_ref[...]
-    for copy in outs:
-        copy.wait()
-    landed(res.at[0], s_res.at[0])
-    sends.finish()
+            logits = logits + dot_nt(w, g)
+    logits = logits + br_ref[...]
+    for r in range(n_req):
+        logit_out[r] = logits[:, r * new:(r + 1) * new]
 
 
 def dma(*shape):
@@ -666,13 +711,9 @@
         wide = w_qkv.shape[1] // row
         ow = model // row
         flat = tokens.reshape(n_tok, model)
-        cs = jnp.concatenate([rope_cos, rope_sin], axis=-1).reshape(n_tok, head)
         core = lax.rem(lax.axis_index(AXIS), CORES)
         bias_pad = lax.dynamic_update_slice(jnp.zeros((3 * head,), F32), b_qkv.astype(F32), (core * b_qkv.shape[0],))
-        pack = jnp.concatenate([
-            norm_attn.astype(F32)[None], b_out.astype(F32)[None], norm_router.astype(F32)[None],
-            bias_pad.reshape(3, head), jnp.zeros((2, head), F32), w_router.astype(F32).T], axis=0)
-        n_pack = pack.shape[0]
+        n_pack = 8 + experts
 
         pieces = 4
         turn = 256
@@ -685,7 +726,7 @@
                        jax.ShapeDtypeStruct((row, depth, ow), BF16),
                        jax.ShapeDtypeStruct((n_req, kv, slots, head), BF16),
                        jax.ShapeDtypeStruct((n_req, kv, slots, head), BF16)),
-            in_specs=[hbm, hbm, hbm, vmem, vmem, hbm, hbm],
+            in_specs=[hbm, hbm, hbm] + [vmem] * 7 + [hbm, hbm],
             out_specs=(hbm,) * 6,
             scratch_shapes=[
                 pltpu.VMEM((row - 1, depth, wide), BF16),
@@ -697,46 +738,56 @@
                 pltpu.VMEM((side, row, n_pack, head), F32),
                 pltpu.VMEM((side, CORES * n_tok, wide), F32),
                 pltpu.VMEM((row, n_tok, wide), BF16),
-                pltpu.VMEM((4, turn, kv, head), BF16), pltpu.VMEM((4, turn, kv, head), BF16),
-                pltpu.VMEM((4, kv, turn, head), BF16), pltpu.VMEM((4, kv, turn, head), BF16),
-                dma(row), dma(row), dma(4), dma(row), dma(row), dma(row), dma(row), dma(row), dma(row),
-                dma(row), dma(row), dma(row), dma(row), dma(3), dma(3),
-                dma(pieces), dma(pieces), dma(pieces), dma(pieces), dma(pieces), dma(pieces), dma(4 * pieces), dma(4 * pieces),
-                dma(row), dma(row), dma(row), dma(row), dma(row), dma(row), dma(row), dma(row), dma(8), dma(8)],
+                *[pltpu.VMEM((pieces, turn, kv, head), BF16)] * 2, *[pltpu.VMEM((pieces, kv, turn, head), BF16)] * 2,
+                pltpu.VMEM((2, depth, wide), BF16), *[pltpu.VMEM((2, depth, ow), BF16)] * 2,
+                pltpu.VMEM((2, n_tok, wide), BF16),
+                *[dma(row)] * 2, dma(pieces), *[dma(row)] * 8, *[dma(side)] * 2,
+                *[dma(pieces)] * 6, *[dma(side * pieces)] * 2, *[dma(2)] * 6, *[dma(2 * side)] * 2,
+                *[dma(row)] * 8, *[dma(2 * pieces)] * 2, *[dma(3, 2)] * 4],
             compiler_params=pltpu.CompilerParams(collective_id=0, has_side_effects=True, vmem_limit_bytes=60 * 2**20),
             name='project',
-        )(w_qkv, w_out, flat, cs, pack, k_cache, v_cache)
+        )(w_qkv, w_out, flat, rope_cos.reshape(n_tok, head // 2), rope_sin.reshape(n_tok, head // 2),
+          norm_attn.reshape(1, head), b_out.reshape(1, head), norm_router.reshape(1, head),
+          bias_pad.reshape(3, head), w_router.T, k_cache, v_cache)
 
         n_row = heads // kv * n_new
-        resid, logits = pl.pallas_call(
-            functools.partial(output_kernel, side, kv, experts),
-            out_shape=(jax.ShapeDtypeStruct((n_tok, model), BF16), jax.ShapeDtypeStruct((n_tok, experts), F32)),
-            in_specs=[smem, smem, vmem, hbm, hbm, hbm, hbm, vmem, vmem],
-            out_specs=(hbm, vmem),
+        parts = 4 * n_req
+        own = pl.pallas_call(
+            functools.partial(output_kernel, side, kv),
+            out_shape=jax.ShapeDtypeStruct((row, n_tok, ow), BF16),
+            in_specs=[smem, smem, vmem, hbm, hbm, hbm, hbm, vmem],
+            out_specs=hbm,
             scratch_shapes=[
-                pltpu.VMEM((slots, head), BF16), pltpu.VMEM((slots, head), BF16),
-                pltpu.VMEM((slots, head), BF16), pltpu.VMEM((slots, head), BF16),
-                pltpu.VMEM((n_row, slots + head), F32), pltpu.VMEM((n_row, slots + head), F32),
-                pltpu.VMEM((n_row, head), F32), pltpu.VMEM((n_row, head), F32),
-                pltpu.VMEM((n_row, head), F32), pltpu.VMEM((n_row, head), F32),
+                *[pltpu.VMEM((slots, head), BF16)] * 4, *[pltpu.VMEM((n_row, slots + head), F32)] * 2,
+                *[pltpu.VMEM((n_row, head), F32)] * 4,
                 pltpu.VMEM((row, n_tok, model), BF16),
                 pltpu.VMEM((side, row, depth, ow), BF16),
                 pltpu.VMEM((row, n_tok, ow), BF16),
                 pltpu.VMEM((side, CORES * n_tok, ow), F32),
                 pltpu.VMEM((row, n_tok, ow), BF16),
-                pltpu.VMEM((row, n_tok, ow), BF16),
-                dma(2), dma(2), dma(3 + row),
-                dma(pieces), dma(pieces), dma(pieces), dma(pieces), dma(pieces), dma(pieces), dma(4 * pieces), dma(4 * pieces),
-                dma(row), dma(row), dma(row), dma(row), dma(row), dma(row), dma(row), dma(row)],
+                pltpu.VMEM((2, n_tok, ow), BF16),
+                *[dma(2)] * 3, *[dma(parts)] * 6, *[dma(side * parts)] * 2, *[dma(row)] * 8, dma(3, 2)],
             compiler_params=pltpu.CompilerParams(collective_id=1, has_side_effects=True, vmem_limit_bytes=56 * 2**20),
             name='output',
-        )(prefix_len, sink_logits, qkv, kt, vt, wo, xb, packs, b_router.reshape(1, experts))
-
-        split = qkv.reshape(row, n_req, n_new, wide)
+        )(prefix_len, sink_logits, qkv, kt, vt, wo, xb, packs)
+
         gw = wide - 2 * head
-        k_new = jnp.transpose(split[..., gw:gw + head], (1, 2, 0, 3))
-        v_new = jnp.transpose(split[..., gw + head:], (1, 2, 0, 3))
-        return (resid.reshape(n_req, n_new, model), logits.reshape(n_req, n_new, experts), k_new, v_new)
+        resid, logits, k_new, v_new = pl.pallas_call(
+            close_kernel,
+            grid=(1,),
+            out_shape=(jax.ShapeDtypeStruct((n_tok, model), BF16), jax.ShapeDtypeStruct((n_req, experts, n_new), F32),
+                       jax.ShapeDtypeStruct((n_req, n_new, kv, head), BF16),
+                       jax.ShapeDtypeStruct((n_req, n_new, kv, head), BF16)),
+            in_specs=[pl.BlockSpec((row, n_tok, ow), lambda i: (0, 0, 0)),
+                      pl.BlockSpec((row, n_tok, 2 * head), lambda i: (0, 0, gw // (2 * head))),
+                      pl.BlockSpec((side, row, n_pack, head), lambda i: (0, 0, 0, 0)),
+                      pl.BlockSpec((experts, 1), lambda i: (0, 0))],
+            out_specs=(pl.BlockSpec((n_tok, model), lambda i: (0, 0)), pl.BlockSpec((n_req, experts, n_new), lambda i: (0, 0, 0)),
+                       pl.BlockSpec((n_req, n_new, kv, head), lambda i: (0, 0, 0, 0)),
+                       pl.BlockSpec((n_req, n_new, kv, head), lambda i: (0, 0, 0, 0))),
+            name='close',
+        )(own, qkv, packs, b_router.reshape(experts, 1))
+        return (resid.reshape(n_req, n_new, model), jnp.transpose(logits, (0, 2, 1)), k_new, v_new)
 
     in_specs = (row_spec, row_spec, row_spec, row_spec, row_spec, row_spec, shard_spec, shard_spec, shard_spec, whole_spec, shard_spec, shard_spec, shard_spec, shard_spec, whole_spec)
     out_specs = (row_spec, row_spec, row_spec, row_spec)

time: 174 us -> 160 us (0.920)
  local copies, waits for them, and re-layouts: 7.82 us -> 1.26 us
  Pallas kernels: 161 us -> 157 us
  other arithmetic: 4.34 us -> 0.75 us
    unnamed x4, local copies, waits for them, and re-layouts: 5.55 us -> 0.58 us
    pallas_call x1, Pallas kernels: 94.8 us -> 91.1 us  [local_step(): pl.pallas_call(functools.partial(project_kernel, side, heads, kv), out_sh...]
    pallas_call x1 -> x2, Pallas kernels: 66 us -> 66.3 us  [the longest x1 62.8 us: local_step(): pl.pallas_call(functools.partial(output_kernel, side, kv), out_shape=jax....]
where the time goes in v3:
time: 160 us
  Pallas kernels  157 us (98%)
    pallas_call x1, Pallas kernels, local_step(): pl.pallas_call(functools.partial(project_kernel, side, heads, kv), out_sh...  91.1 us
    pallas_call x1, Pallas kernels, local_step(): pl.pallas_call(functools.partial(output_kernel, side, kv), out_shape=jax....  62.8 us
    pallas_call x1, Pallas kernels, local_step(): pl.pallas_call(close_kernel, grid=(1,), out_shape=(jax.ShapeDtypeStruct((...  3.52 us

profile of v3, /device:TPU:97, one launch (start us, length us, event | category | flops | bytes accessed | tf_op | source)
XLA Modules:
  0.0 160.1 jit_solution(3156363663164796904)
XLA Ops:
  0.7 0.8 convert_dynamic-update-slice_fusion
  1.4 0.0 copy-start
  1.4 0.6 copy-done
  2.0 91.1 %project.1 = (bf16[8,128,768]{2,1,0:T(8,128)(2,1)}, bf16[8,128,512]{2,1,0:T(8,128)(2,1)}, f32[4,8,16,128]{3,2,1,0:T(8,128)}, bf16[8,128,512]{2,1,0:T(8,128)(2,1)...) custom-call(bf16[128,6144]{1,0:T(8,128)(2,1)} %w_ref.1, bf16[128,4096]{1,0:T(8,128)(2,1)} %wo_ref.1, ...), custom_call_target="tpu_custom_call" | custom-call | tf_op jit(solution)/shard_map/project/pallas_call | solution.py:721
  93.1 0.0 copy-start.1
  93.1 62.8 %output.1.own = bf16[8,128,512]{2,1,0:T(8,128)(2,1)} custom-call(s32[2]{0:T(128)} %len_ref.1, f32[32]{0:T(128)} %sink_ref.1, bf16[8,128,768]{2,1,0:T(8,128)(2,1)} %get-tuple-element.14.qkv_ref, bf16[2,8,4096,128]{3,2,1,0:T(8,128)(2,1)} %get-tuple-element.15.kt_ref, bf16[2,8,4096,128]{3,2,1,0:T(8,128)(2,1)} %get-tuple-element.16.vt_ref, ...), custom_call_target="tpu_custom_call" | custom-call | tf_op jit(solution)/shard_map/output/pallas_call | solution.py:755
  155.9 0.0 copy-done.1
  156.0 0.7 copy.19.br_ref
  156.6 3.5 %close.1 = (bf16[128,4096]{1,0:T(8,128)(2,1)}, f32[2,8,64]{2,1,0:T(8,128)}, bf16[2,64,8,128]{3,2,1,0:T(8,128)(2,1)}, bf16[2,64,8,128]{3,2,1,0:T(8,128)(2,1)}) custom-call(bf16[8,128,512]{2,1,0:T(8,128)(2,1)} %output.1.own, bf16[8,128,768]{2,1,0:T(8,128)(2,1)} %get-tuple-element.14.qkv_ref, f32[4,8,16,128]{3,2,1,0:T(8,128)} %get-tuple-element.19.packs, ...), custom_call_target="tpu_custom_call" | custom-call | tf_op jit(solution)/shard_map/close/pallas_call | solution.py:775
  (1 shorter events, 0.0 us)
Async XLA Ops:
  1.4 0.6 copy-start
  93.1 62.9 %copy-start.1 = (f32[8]{0:T(128)S(1)}, f32[8]{0:T(128)}, u32[]{:S(2)}) copy-start(f32[8]{0:T(128)} %param.29) | copy-start | bytes 100

commit v4 on v3

--- a/solution.py
+++ b/solution.py
@@ -412,25 +412,27 @@
         acc[da] = part(da, 0)
         acc[da] += part(da, 1)
         acc[da] += part(da, back)
-    for k in range(count):
+    for da in range(side):
+        tables.from_pair(da)
+    for k in range(count // 2):
+        tokens.far(k)
+    for k in range(row):
+        gather.far(k)
+    finish(1)
+    finish(back)
+    for k in range(count // 2, count):
         tokens.far(k)
     norm(p.spot(2))
     tokens.from_pair(2)
     norm(p.spot(2, OTHER))
-    for da in range(side):
-        tables.from_pair(da)
     acc[2] = part(2, 0)
     acc[2] += part(2, 1)
     acc[2] += part(2, back)
-    for k in range(row):
-        gather.far(k)
     finish(2)
-    finish(1)
-    finish(back)
-    swap_r.hand()
     swap_o.hand()
     finish(0)
     swap_x.hand()
+    swap_r.hand()
     for at in rel:
         swap_o.arrived(*at)
         swap_x.arrived(*at)
@@ -446,7 +448,7 @@
 
 
 def output_kernel(side, kv, len_ref, sink_ref, qkv_ref, kt_ref, vt_ref, wo_ref, xb_ref, packs, own,
-                  kb0, kb1, vb0, vb1, sb0, sb1, mb0, mb1, lb0, lb1, oa, wq, xbv, acc, res, pass_r,
+                  kb, vb, sb0, sb1, mb0, mb1, lb0, lb1, oa, wq, xbv, acc, res, pass_r,
                   s_k, s_v, s_loc, s_plus, r_plus, s_minus, r_minus, s_rfar, r_rfar, s_pair, r_pair,
                   s_up, r_up, s_dn, r_dn, s_far, r_far, s_res, r_res, h_r):
     p = Place(side, across=True)
@@ -470,14 +472,28 @@
     for copy in loads:
         copy.start()
 
+    deep = kb.shape[0]
+    quarter = slots // deep
+
     def fetch(n, which, buf, sem):
-        n = jnp.minimum(n, total - 1)
-        return pltpu.make_async_copy(which.at[n // kv, lax.rem(n, kv)], buf, sem)
-
-    fetch(0, kt_ref, kb0, s_k.at[0]).start()
-    fetch(0, vt_ref, vb0, s_v.at[0]).start()
-    fetch(1, kt_ref, kb1, s_k.at[1]).start()
-    fetch(1, vt_ref, vb1, s_v.at[1]).start()
+        slot = lax.rem(n, deep)
+
+        @pl.when(n < total)
+        def _():
+            for k in range(deep):
+                at = pl.ds(k * quarter, quarter)
+                pltpu.make_async_copy(which.at[n // kv, lax.rem(n, kv), at], buf.at[slot, at], sem.at[slot]).start()
+
+    def fetched(n, buf, sem):
+        slot = lax.rem(n, deep)
+
+        @pl.when(n < total)
+        def _():
+            landed(buf.at[slot], sem.at[slot])
+
+    for n in range(deep):
+        fetch(jnp.int32(n), kt_ref, kb, s_k)
+        fetch(jnp.int32(n), vt_ref, vb, s_v)
     meet(p.mates() + [p.above(1), p.above(back)])
     gather = ColumnGather(p, sends, wq, (s_up, r_up), (s_dn, r_dn), (s_far, r_far))
     count = r_plus.shape[0]
@@ -500,7 +516,8 @@
     ri = lax.rem(lax.broadcasted_iota(jnp.int32, (rows, head), 0), new)
     ci = lax.broadcasted_iota(jnp.int32, (rows, head), 1)
 
-    def first(n, sb, mb, lb, kb):
+    def first(n, sb, mb, lb):
+        slot = lax.rem(n, deep)
         n = jnp.minimum(n, total - 1)
         r, i = n // kv, lax.rem(n, kv)
         q = jnp.concatenate([qkv_ref[i, place(r), g * head:(g + 1) * head] for g in range(group)], axis=0)
@@ -511,7 +528,7 @@
         sb[:, slots:] = s
         m = s
         for b in range(slots // block):
-            s = dot_nt(q, kb[b * block:(b + 1) * block])
+            s = dot_nt(q, kb[slot, b * block:(b + 1) * block])
             s = jnp.where(b * block + lax.broadcasted_iota(jnp.int32, (1, block), 1) < length, s, -1e30)
             sb[:, b * block:(b + 1) * block] = s
             for k in range(block // head):
@@ -523,7 +540,8 @@
         mb[...] = m
         lb[...] = jnp.exp2(sink - m)
 
-    def second(n, sb, mb, lb, vb):
+    def second(n, sb, mb, lb):
+        slot = lax.rem(n, deep)
         r, i = n // kv, lax.rem(n, kv)
         m = mb[...]
         vn = qkv_ref[i, place(r), (group + 1) * head:]
@@ -538,7 +556,7 @@
                 pr = jnp.exp2(sb[:, at:at + head] * scale - m)
                 low = low + pr
                 prs.append(pr.astype(BF16))
-            out = out + jnp.dot(jnp.concatenate(prs, axis=1), vb[b * block:(b + 1) * block], preferred_element_type=F32)
+            out = out + jnp.dot(jnp.concatenate(prs, axis=1), vb[slot, b * block:(b + 1) * block], preferred_element_type=F32)
             yield
         out = (out / (jnp.sum(low, axis=-1, keepdims=True) + lb[...])).astype(BF16)
         for g in range(group):
@@ -552,9 +570,9 @@
                 if next(w, w) is w:
                     work.remove(w)
 
-    fetch(0, kt_ref, kb0, s_k.at[0]).wait()
-    run(first(0, sb0, mb0, lb0, kb0))
-    fetch(2, kt_ref, kb0, s_k.at[0]).start()
+    fetched(jnp.int32(0), kb, s_k)
+    run(first(jnp.int32(0), sb0, mb0, lb0))
+    fetch(jnp.int32(deep), kt_ref, kb, s_k)
     turns = total // 2
     each = turns // count
 
@@ -574,17 +592,12 @@
         return out
 
     def body(h, _):
-        n = 2 * h
-        fetch(n, vt_ref, vb0, s_v.at[0]).wait()
-        fetch(n + 1, kt_ref, kb1, s_k.at[1]).wait()
-        run(first(n + 1, sb1, mb1, lb1, kb1), second(n, sb0, mb0, lb0, vb0))
-        fetch(n + 2, vt_ref, vb0, s_v.at[0]).start()
-        fetch(n + 3, kt_ref, kb1, s_k.at[1]).start()
-        fetch(n + 1, vt_ref, vb1, s_v.at[1]).wait()
-        fetch(n + 2, kt_ref, kb0, s_k.at[0]).wait()
-        run(first(n + 2, sb0, mb0, lb0, kb0), second(n + 1, sb1, mb1, lb1, vb1))
-        fetch(n + 3, vt_ref, vb1, s_v.at[1]).start()
-        fetch(n + 4, kt_ref, kb0, s_k.at[0]).start()
+        for n, one, two in ((2 * h, (sb1, mb1, lb1), (sb0, mb0, lb0)), (2 * h + 1, (sb0, mb0, lb0), (sb1, mb1, lb1))):
+            fetched(n, vb, s_v)
+            fetched(n + 1, kb, s_k)
+            run(first(n + 1, *one), second(n, *two))
+            fetch(n + deep, vt_ref, vb, s_v)
+            fetch(n + deep + 1, kt_ref, kb, s_k)
         for at in range(turns):
             todo = events(at)
             if todo:
@@ -595,8 +608,6 @@
         return 0
 
     lax.fori_loop(0, turns, body, 0)
-    for which, buf, sem in ((vt_ref, vb0, s_v.at[0]), (vt_ref, vb1, s_v.at[1]), (kt_ref, kb0, s_k.at[0]), (kt_ref, kb1, s_k.at[1])):
-        fetch(0, which, buf, sem).wait()
     past = [e for h in range(turns) for e in events(h)]
 
     def rest(act, k):
@@ -758,7 +769,7 @@
             in_specs=[smem, smem, vmem, hbm, hbm, hbm, hbm, vmem],
             out_specs=hbm,
             scratch_shapes=[
-                *[pltpu.VMEM((slots, head), BF16)] * 4, *[pltpu.VMEM((n_row, slots + head), F32)] * 2,
+                *[pltpu.VMEM((4, slots, head), BF16)] * 2, *[pltpu.VMEM((n_row, slots + head), F32)] * 2,
                 *[pltpu.VMEM((n_row, head), F32)] * 4,
                 pltpu.VMEM((row, n_tok, model), BF16),
                 pltpu.VMEM((side, row, depth, ow), BF16),
@@ -766,7 +777,7 @@
                 pltpu.VMEM((side, CORES * n_tok, ow), F32),
                 pltpu.VMEM((row, n_tok, ow), BF16),
                 pltpu.VMEM((2, n_tok, ow), BF16),
-                *[dma(2)] * 3, *[dma(parts)] * 6, *[dma(side * parts)] * 2, *[dma(row)] * 8, dma(3, 2)],
+                *[dma(4)] * 2, dma(2), *[dma(parts)] * 6, *[dma(side * parts)] * 2, *[dma(row)] * 8, dma(3, 2)],
             compiler_params=pltpu.CompilerParams(collective_id=1, has_side_effects=True, vmem_limit_bytes=56 * 2**20),
             name='output',
         )(prefix_len, sink_logits, qkv, kt, vt, wo, xb, packs)

time: 160 us -> 158 us (0.988)
    pallas_call x1, Pallas kernels: 91.1 us -> 89.2 us  [local_step(): pl.pallas_call(functools.partial(project_kernel, side, heads, kv), out_sh...]
where the time goes in v4:
time: 158 us
  Pallas kernels  156 us (99%)
    pallas_call x1, Pallas kernels, local_step(): pl.pallas_call(functools.partial(project_kernel, side, heads, kv), out_sh...  89.2 us
    pallas_call x1, Pallas kernels, local_step(): pl.pallas_call(functools.partial(output_kernel, side, kv), out_shape=jax....  62.8 us
    pallas_call x1, Pallas kernels, local_step(): pl.pallas_call(close_kernel, grid=(1,), out_shape=(jax.ShapeDtypeStruct((...  3.52 us

profile of v4, /device:TPU:97, one launch (start us, length us, event | category | flops | bytes accessed | tf_op | source)
XLA Modules:
  0.0 158.2 jit_solution(1292950682724352041)
XLA Ops:
  0.7 0.8 convert_dynamic-update-slice_fusion
  1.4 0.0 copy-start
  1.4 0.6 copy-done
  2.0 89.2 %project.1 = (bf16[8,128,768]{2,1,0:T(8,128)(2,1)}, bf16[8,128,512]{2,1,0:T(8,128)(2,1)}, f32[4,8,16,128]{3,2,1,0:T(8,128)}, bf16[8,128,512]{2,1,0:T(8,128)(2,1)...) custom-call(bf16[128,6144]{1,0:T(8,128)(2,1)} %w_ref.1, bf16[128,4096]{1,0:T(8,128)(2,1)} %wo_ref.1, ...), custom_call_target="tpu_custom_call" | custom-call | tf_op jit(solution)/shard_map/project/pallas_call | solution.py:732
  91.2 0.0 copy-start.1
  91.2 62.8 %output.1.own = bf16[8,128,512]{2,1,0:T(8,128)(2,1)} custom-call(s32[2]{0:T(128)} %len_ref.1, f32[32]{0:T(128)} %sink_ref.1, bf16[8,128,768]{2,1,0:T(8,128)(2,1)} %get-tuple-element.14.qkv_ref, bf16[2,8,4096,128]{3,2,1,0:T(8,128)(2,1)} %get-tuple-element.15.kt_ref, bf16[2,8,4096,128]{3,2,1,0:T(8,128)(2,1)} %get-tuple-element.16.vt_ref, ...), custom_call_target="tpu_custom_call" | custom-call | tf_op jit(solution)/shard_map/output/pallas_call | solution.py:766
  154.0 0.0 copy-done.1
  154.0 0.7 copy.19.br_ref
  154.7 3.5 %close.1 = (bf16[128,4096]{1,0:T(8,128)(2,1)}, f32[2,8,64]{2,1,0:T(8,128)}, bf16[2,64,8,128]{3,2,1,0:T(8,128)(2,1)}, bf16[2,64,8,128]{3,2,1,0:T(8,128)(2,1)}) custom-call(bf16[8,128,512]{2,1,0:T(8,128)(2,1)} %output.1.own, bf16[8,128,768]{2,1,0:T(8,128)(2,1)} %get-tuple-element.14.qkv_ref, f32[4,8,16,128]{3,2,1,0:T(8,128)} %get-tuple-element.19.packs, ...), custom_call_target="tpu_custom_call" | custom-call | tf_op jit(solution)/shard_map/close/pallas_call | solution.py:786
  (1 shorter events, 0.0 us)
Async XLA Ops:
  1.4 0.6 copy-start
  91.2 62.8 %copy-start.1 = (f32[8]{0:T(128)S(1)}, f32[8]{0:T(128)}, u32[]{:S(2)}) copy-start(f32[8]{0:T(128)} %param.29) | copy-start | bytes 100

commit v5 on v4

--- a/solution.py
+++ b/solution.py
@@ -583,7 +583,7 @@
         for k in range(count):
             if h == (k + 1) * each + 2:
                 out.append((tokens.near, k))
-            if h == (k + 1) * each + 4:
+            if h == (k + 1) * each + 5:
                 out.append((tokens.far, k))
         if h >= turns // 2:
             for k in range(row):
@@ -641,18 +641,19 @@
         rest(gather.near, k)
     for k in range(count):
         rest(tokens.near, k)
-        if k > 1:
-            rest(tokens.far, k - 2)
+    for k in range(count // 2):
+        rest(tokens.far, k)
     for da in (back, 1):
         tokens.from_pair(da)
         acc[da] = part(da, 0)
         acc[da] += part(da, 1)
         acc[da] += part(da, back)
-        rest(tokens.far, count - 2 if da == back else count - 1)
     for k in range(row):
         gather.far(k)
     finish(1)
     finish(back)
+    for k in range(count // 2, count):
+        rest(tokens.far, k)
     tokens.from_pair(2)
     acc[2] = part(2, 0)
     acc[2] += part(2, 1)

time: 158 us -> 156 us (0.987)
  Pallas kernels: 156 us -> 153 us
    pallas_call x1, Pallas kernels: 62.8 us -> 60 us  [local_step(): pl.pallas_call(functools.partial(output_kernel, side, kv), out_shape=jax....]
where the time goes in v5:
time: 156 us; the launch traced here: 155 us
  Pallas kernels  153 us (98%)
    pallas_call x1, Pallas kernels, local_step(): pl.pallas_call(functools.partial(project_kernel, side, heads, kv), out_sh...  89.2 us
    pallas_call x1, Pallas kernels, local_step(): pl.pallas_call(functools.partial(output_kernel, side, kv), out_shape=jax....  60 us
    pallas_call x1, Pallas kernels, local_step(): pl.pallas_call(close_kernel, grid=(1,), out_shape=(jax.ShapeDtypeStruct((...  3.52 us

profile of v5, /device:TPU:97, one launch (start us, length us, event | category | flops | bytes accessed | tf_op | source)
XLA Modules:
  0.0 155.4 jit_solution(15158612683527143442)
XLA Ops:
  0.7 0.8 convert_dynamic-update-slice_fusion
  1.4 0.0 copy-start
  1.4 0.6 copy-done
  2.0 89.2 %project.1 = (bf16[8,128,768]{2,1,0:T(8,128)(2,1)}, bf16[8,128,512]{2,1,0:T(8,128)(2,1)}, f32[4,8,16,128]{3,2,1,0:T(8,128)}, bf16[8,128,512]{2,1,0:T(8,128)(2,1)...) custom-call(bf16[128,6144]{1,0:T(8,128)(2,1)} %w_ref.1, bf16[128,4096]{1,0:T(8,128)(2,1)} %wo_ref.1, ...), custom_call_target="tpu_custom_call" | custom-call | tf_op jit(solution)/shard_map/project/pallas_call | solution.py:733
  91.2 0.0 copy-start.1
  91.2 60.0 %output.1.own = bf16[8,128,512]{2,1,0:T(8,128)(2,1)} custom-call(s32[2]{0:T(128)} %len_ref.1, f32[32]{0:T(128)} %sink_ref.1, bf16[8,128,768]{2,1,0:T(8,128)(2,1)} %get-tuple-element.14.qkv_ref, bf16[2,8,4096,128]{3,2,1,0:T(8,128)(2,1)} %get-tuple-element.15.kt_ref, bf16[2,8,4096,128]{3,2,1,0:T(8,128)(2,1)} %get-tuple-element.16.vt_ref, ...), custom_call_target="tpu_custom_call" | custom-call | tf_op jit(solution)/shard_map/output/pallas_call | solution.py:767
  151.2 0.0 copy-done.1
  151.2 0.7 copy.19.br_ref
  151.9 3.5 %close.1 = (bf16[128,4096]{1,0:T(8,128)(2,1)}, f32[2,8,64]{2,1,0:T(8,128)}, bf16[2,64,8,128]{3,2,1,0:T(8,128)(2,1)}, bf16[2,64,8,128]{3,2,1,0:T(8,128)(2,1)}) custom-call(bf16[8,128,512]{2,1,0:T(8,128)(2,1)} %output.1.own, bf16[8,128,768]{2,1,0:T(8,128)(2,1)} %get-tuple-element.14.qkv_ref, f32[4,8,16,128]{3,2,1,0:T(8,128)} %get-tuple-element.19.packs, ...), custom_call_target="tpu_custom_call" | custom-call | tf_op jit(solution)/shard_map/close/pallas_call | solution.py:787
  (1 shorter events, 0.0 us)
Async XLA Ops:
  1.4 0.6 copy-start
  91.2 60.0 %copy-start.1 = (f32[8]{0:T(128)S(1)}, f32[8]{0:T(128)}, u32[]{:S(2)}) copy-start(f32[8]{0:T(128)} %param.29) | copy-start | bytes 100
